TPU v7x, 32 devices: a whole 2x2x4 slice. The times are simulated.
32 devices in a mesh: tm: 8 (over z, y), space: 4 (over x, core).
Axes of the slice: x: 2, y: 2, z: 4, core: 2. Of those that a mesh axis runs over, the one named last changes fastest.
Arguments:
- source: float32 [8, 32, 128, 128], P('tm', 'space'), may hold values from -8 to 8
- conductivity: float32 [32, 128, 128], P('space'), may hold values from 0.5 to 4
Outputs:
- solution: float32 [8, 32, 128, 128], P('tm', 'space')
- final_defect: float32 [8, 32, 128, 128], P('tm', 'space')
All inputs are finite; a program needn't handle non-finite values.
Results may differ from a plain program's by a relative error of at most 0.000034.
Values sent between devices are 32-bit elements; how exact they have to be, the bound alone decides.
A program may use at most 64 MiB of HBM per device.

v0:
```python
import jax
import jax.numpy as jnp
from jax import lax
from jax.sharding import PartitionSpec as P

NU = 2
NC = 4


OMEGA = 0.8
FINE = (1.0, 1.0, 1.0)
COARSE = (0.25, 0.25, 1.0)


def padded_2(shard, sides, width):
    for axis, dim in sides:
        peers, length = (lax.axis_size(axis), shard.shape[dim])
        up = [(i, (i + 1) % peers) for i in range(peers - 1)]
        down = [(j, i) for i, j in up]
        last = lax.slice_in_dim(shard, length - width, length, axis=dim)
        first = lax.slice_in_dim(shard, 0, width, axis=dim)
        before = lax.ppermute(last, axis, up)
        after = lax.ppermute(first, axis, down)
        shard = jnp.concatenate([before, shard, after], axis=dim)
    return shard


def shifted(shard, axis, by):
    peers = lax.axis_size(axis)
    pairs = [(i, i + by) for i in range(peers) if 0 <= i + by < peers]
    return lax.ppermute(shard, axis, pairs)


def swapped(value, axis, bit):
    mask = 2**bit
    pairs = [(source, source ^ mask) for source in range(lax.axis_size(axis))]
    return lax.ppermute(value, axis, pairs)


def stencil(padded, weights):
    weight_z, weight_x, weight_y = weights
    centre = padded[1:-1, :, 1:-1]
    widened = jnp.pad(padded[1:-1], ((0, 0), (1, 1), (0, 0)))
    along_z = 2.0 * centre - padded[2:, :, 1:-1] - padded[:-2, :, 1:-1]
    along_x = 2.0 * centre - widened[:, 2:, 1:-1] - widened[:, :-2, 1:-1]
    along_y = 2.0 * centre - padded[1:-1, :, 2:] - padded[1:-1, :, :-2]
    return weight_z * along_z + weight_x * along_x + weight_y * along_y


def defect(current, right_side, earlier, padded, conduct, stretch, weights):
    applied = current + stretch * conduct * stencil(padded, weights)
    return right_side + earlier - applied


def relaxed(current, right_side, earlier, padded, conduct, stretch, weights):
    weight_sum = 2.0 * (weights[0] + weights[1] + weights[2])
    diagonal = 1.0 + stretch * conduct * weight_sum
    return (
        current
        + OMEGA * defect(current, right_side, earlier, padded, conduct, stretch, weights) / diagonal
    )


def coarsen(values):
    return 0.25 * (
        values[..., 0::2, 0::2, :]
        + values[..., 1::2, 0::2, :]
        + (values[..., 0::2, 1::2, :] + values[..., 1::2, 1::2, :])
    )


def refine(values):
    return jnp.repeat(jnp.repeat(values, 2, axis=-3), 2, axis=-2)


def zero_columns(values):
    return jnp.pad(values, ((0, 0), (0, 0), (1, 1)))


def plane_faces(values):
    return padded_2(values, (("space", 0),), 1)


def coarse_planes_framed(values):
    return padded_2(values, (("space", 0),), 1)


def fine_frame(values):
    return zero_columns(plane_faces(values))


def step_prior(values):
    return shifted(values, "tm", 1)


def pair_prior(values):
    return shifted(values, "tm", 2)


def group_prior(values):
    return shifted(values, "tm", 4)


def smooth(current, right_side, conduct, stretch, weights, repeats, earlier_of, framing):
    for turn_index in range(repeats):
        current = relaxed(
            current, right_side, earlier_of(current), framing(current), conduct, stretch, weights
        )
    return current


def body(source, conductivity):
    right_side = source[0]
    solution = smooth(
        jnp.zeros_like(right_side), right_side, conductivity, 1.0, FINE, NU, step_prior, fine_frame
    )
    defect_fine = defect(
        solution, right_side, step_prior(solution), fine_frame(solution), conductivity, 1.0, FINE
    )
    middle_full = defect_fine + swapped(defect_fine, "tm", 0)
    middle = smooth(
        jnp.zeros_like(middle_full),
        middle_full,
        conductivity,
        2.0,
        FINE,
        NU,
        pair_prior,
        fine_frame,
    )
    middle_defect = defect(
        middle, middle_full, pair_prior(middle), fine_frame(middle), conductivity, 2.0, FINE
    )
    summed = middle_defect + swapped(middle_defect, "tm", 1)
    coarse_rhs = coarsen(summed)
    coarse_cond = coarsen(conductivity)

    def coarse_frame(values):
        return zero_columns(coarse_planes_framed(values))

    coarse = smooth(
        jnp.zeros_like(coarse_rhs),
        coarse_rhs,
        coarse_cond,
        4.0,
        COARSE,
        NC,
        group_prior,
        coarse_frame,
    )
    middle = middle + refine(coarse)
    middle = smooth(middle, middle_full, conductivity, 2.0, FINE, NU, pair_prior, fine_frame)
    solution = solution + middle
    solution = smooth(solution, right_side, conductivity, 1.0, FINE, NU, step_prior, fine_frame)
    final_defect = defect(
        solution, right_side, step_prior(solution), fine_frame(solution), conductivity, 1.0, FINE
    )
    return (solution[None], final_defect[None])


def solution(mesh):
    return jax.shard_map(
        body,
        mesh=mesh,
        in_specs=(P("tm", "space", None, None), P("space", None, None)),
        out_specs=(P("tm", "space", None, None), P("tm", "space", None, None)),
        check_vma=False,
    )
```

profile of v0, /device:TPU:0, one launch (start us, length us, event | category | flops | bytes accessed | tf_op | source)
XLA Modules:
  0.0 235.4 jit_solution(14817165002886367265)
XLA Ops:
  0.7 4.9 %collective-permute-start = (f32[8,128,128]{2,1,0:T(8,128)S(1)}, f32[8,128,128]{2,1,0:T(8,128)S(1)}, u32[]{:S(2)}, u32[]{:S(2)}) collective-permute-start(f32[8,128,128]{2,1,0:T(8,128)S(1)} %slice.484), channel_id=1, source_target_pairs={{0,4},{4,8},{8,12},{12,16},{16,20},{20,24},{24,28},{1,5},{5,9},{9,... | collective-permute-start | bytes 1572872 | tf_op jit(solution)/shard_map/ppermute | solution.py:31
  6.9 3.0 %collective-permute-start.2 = (f32[1,128,128]{2,1,0:T(8,128)S(1)}, f32[1,128,128]{2,1,0:T(8,128)S(1)}, u32[]{:S(2)}, u32[]{:S(2)}) collective-permute-start(f32[1,128,128]{2,1,0:T(8,128)S(1)} %broadcast.105), channel_id=1, source_target_pairs={{0,1},{1,2},{2,3},{4,5},{5,6},{6,7},{8,9},{9,10},{10,11},{12,13},{... | collective-permute-start | bytes 196616 | tf_op jit(solution)/shard_map/ppermute | solution.py:22
  11.4 5.4 %collective-permute-done = f32[8,128,128]{2,1,0:T(8,128)S(1)} collective-permute-done((f32[8,128,128]{2,1,0:T(8,128)S(1)}, f32[8,128,128]{2,1,0:T(8,128)S(1)}, u32[]{:S(2)}, u32[]{:S(2)}) %collective-permute-start) | collective-permute-done | bytes 524320 | tf_op jit(solution)/shard_map/ppermute | solution.py:31
  17.3 4.4 %collective-permute-start.3 = (f32[8,128,128]{2,1,0:T(8,128)S(1)}, f32[8,128,128]{2,1,0:T(8,128)S(1)}, u32[]{:S(2)}, u32[]{:S(2)}) collective-permute-start(f32[8,128,128]{2,1,0:T(8,128)S(1)} %get-tuple-element.7), channel_id=1, source_target_pairs={{0,4},{4,8},{8,12},{12,16},{16,20},{20,24},{24,28},{1,5},{5,9},{9,... | collective-permute-start | bytes 1572872 | tf_op jit(solution)/shard_map/ppermute | solution.py:31
  23.1 3.0 %collective-permute-start.5 = (f32[1,128,128]{2,1,0:T(8,128)S(1)}, f32[1,128,128]{2,1,0:T(8,128)S(1)}, u32[]{:S(2)}, u32[]{:S(2)}) collective-permute-start(f32[1,128,128]{2,1,0:T(8,128)S(1)} %get-tuple-element.25), channel_id=1, source_target_pairs={{0,1},{1,2},{2,3},{4,5},{5,6},{6,7},{8,9},{9,10},{10,11},{12,13},{... | collective-permute-start | bytes 196616 | tf_op jit(solution)/shard_map/ppermute | solution.py:22
  27.5 4.5 %collective-permute-done.3 = f32[8,128,128]{2,1,0:T(8,128)S(1)} collective-permute-done((f32[8,128,128]{2,1,0:T(8,128)S(1)}, f32[8,128,128]{2,1,0:T(8,128)S(1)}, u32[]{:S(2)}, u32[]{:S(2)}) %collective-permute-start.3) | collective-permute-done | bytes 524320 | tf_op jit(solution)/shard_map/ppermute | solution.py:31
  32.7 4.4 %collective-permute-start.6 = (f32[8,128,128]{2,1,0:T(8,128)S(1)}, f32[8,128,128]{2,1,0:T(8,128)S(1)}, u32[]{:S(2)}, u32[]{:S(2)}) collective-permute-start(f32[8,128,128]{2,1,0:T(8,128)S(1)} %fusion.16), channel_id=1, source_target_pairs={{0,4},{4,8},{8,12},{12,16},{16,20},{20,24},{24,28},{1,5},{5,9},{9,... | collective-permute-start | bytes 1572872 | tf_op jit(solution)/shard_map/ppermute | solution.py:31
  38.4 3.0 %collective-permute-start.8 = (f32[1,128,128]{2,1,0:T(8,128)S(1)}, f32[1,128,128]{2,1,0:T(8,128)S(1)}, u32[]{:S(2)}, u32[]{:S(2)}) collective-permute-start(f32[1,128,128]{2,1,0:T(8,128)S(1)} %get-tuple-element.23), channel_id=1, source_target_pairs={{0,1},{1,2},{2,3},{4,5},{5,6},{6,7},{8,9},{9,10},{10,11},{12,13},{... | collective-permute-start | bytes 196616 | tf_op jit(solution)/shard_map/ppermute | solution.py:22
  41.4 3.8 %collective-permute-start.10 = (f32[8,128,128]{2,1,0:T(8,128)S(1)}, f32[8,128,128]{2,1,0:T(8,128)S(1)}, u32[]{:S(2)}, u32[]{:S(2)}) collective-permute-start(f32[8,128,128]{2,1,0:T(8,128)S(1)} %slice.484), channel_id=1, source_target_pairs={{0,8},{4,12},{8,16},{12,20},{16,24},{20,28},{1,9},{5,13},{9,17},{1... | collective-permute-start | bytes 1572872 | tf_op jit(solution)/shard_map/ppermute | solution.py:31
  47.2 3.8 %collective-permute-start.9 = (f32[8,128,128]{2,1,0:T(8,128)S(1)}, f32[8,128,128]{2,1,0:T(8,128)S(1)}, u32[]{:S(2)}, u32[]{:S(2)}) collective-permute-start(f32[8,128,128]{2,1,0:T(8,128)S(1)} %fusion.23), channel_id=1, source_target_pairs={{0,4},{4,0},{8,12},{12,8},{16,20},{20,16},{24,28},{28,24},{1,5},{5... | collective-permute-start | bytes 1572872 | tf_op jit(solution)/shard_map/ppermute | solution.py:37
  51.0 6.4 %collective-permute-done.10 = f32[8,128,128]{2,1,0:T(8,128)S(1)} collective-permute-done((f32[8,128,128]{2,1,0:T(8,128)S(1)}, f32[8,128,128]{2,1,0:T(8,128)S(1)}, u32[]{:S(2)}, u32[]{:S(2)}) %collective-permute-start.10) | collective-permute-done | bytes 524320 | tf_op jit(solution)/shard_map/ppermute | solution.py:31
  57.4 5.1 %collective-permute-done.9 = f32[8,128,128]{2,1,0:T(8,128)S(1)} collective-permute-done((f32[8,128,128]{2,1,0:T(8,128)S(1)}, f32[8,128,128]{2,1,0:T(8,128)S(1)}, u32[]{:S(2)}, u32[]{:S(2)}) %collective-permute-start.9) | collective-permute-done | bytes 524320 | tf_op jit(solution)/shard_map/ppermute | solution.py:37
  62.7 3.5 %collective-permute-start.11 = (f32[8,128,128]{2,1,0:T(8,128)S(1)}, f32[8,128,128]{2,1,0:T(8,128)S(1)}, u32[]{:S(2)}, u32[]{:S(2)}) collective-permute-start(f32[8,128,128]{2,1,0:T(8,128)S(1)} %get-tuple-element.5), channel_id=1, source_target_pairs={{0,8},{4,12},{8,16},{12,20},{16,24},{20,28},{1,9},{5,13},{9,17},{1... | collective-permute-start | bytes 1572872 | tf_op jit(solution)/shard_map/ppermute | solution.py:31
  67.5 3.0 %collective-permute-start.13 = (f32[1,128,128]{2,1,0:T(8,128)S(1)}, f32[1,128,128]{2,1,0:T(8,128)S(1)}, u32[]{:S(2)}, u32[]{:S(2)}) collective-permute-start(f32[1,128,128]{2,1,0:T(8,128)S(1)} %get-tuple-element.21), channel_id=1, source_target_pairs={{0,1},{1,2},{2,3},{4,5},{5,6},{6,7},{8,9},{9,10},{10,11},{12,13},{... | collective-permute-start | bytes 196616 | tf_op jit(solution)/shard_map/ppermute | solution.py:22
  71.9 3.0 %collective-permute-done.11 = f32[8,128,128]{2,1,0:T(8,128)S(1)} collective-permute-done((f32[8,128,128]{2,1,0:T(8,128)S(1)}, f32[8,128,128]{2,1,0:T(8,128)S(1)}, u32[]{:S(2)}, u32[]{:S(2)}) %collective-permute-start.11) | collective-permute-done | bytes 524320 | tf_op jit(solution)/shard_map/ppermute | solution.py:31
  75.5 4.4 %collective-permute-start.14 = (f32[8,128,128]{2,1,0:T(8,128)S(1)}, f32[8,128,128]{2,1,0:T(8,128)S(1)}, u32[]{:S(2)}, u32[]{:S(2)}) collective-permute-start(f32[8,128,128]{2,1,0:T(8,128)S(1)} %fusion.33), channel_id=1, source_target_pairs={{0,8},{4,12},{8,16},{12,20},{16,24},{20,28},{1,9},{5,13},{9,17},{1... | collective-permute-start | bytes 1572872 | tf_op jit(solution)/shard_map/ppermute | solution.py:31
  81.3 3.0 %collective-permute-start.16 = (f32[1,128,128]{2,1,0:T(8,128)S(1)}, f32[1,128,128]{2,1,0:T(8,128)S(1)}, u32[]{:S(2)}, u32[]{:S(2)}) collective-permute-start(f32[1,128,128]{2,1,0:T(8,128)S(1)} %get-tuple-element.19), channel_id=1, source_target_pairs={{0,1},{1,2},{2,3},{4,5},{5,6},{6,7},{8,9},{9,10},{10,11},{12,13},{... | collective-permute-start | bytes 196616 | tf_op jit(solution)/shard_map/ppermute | solution.py:22
  85.7 3.5 %collective-permute-done.14 = f32[8,128,128]{2,1,0:T(8,128)S(1)} collective-permute-done((f32[8,128,128]{2,1,0:T(8,128)S(1)}, f32[8,128,128]{2,1,0:T(8,128)S(1)}, u32[]{:S(2)}, u32[]{:S(2)}) %collective-permute-start.14) | collective-permute-done | bytes 524320 | tf_op jit(solution)/shard_map/ppermute | solution.py:31
  90.0 2.5 %collective-permute-start.17 = (f32[8,128,128]{2,1,0:T(8,128)S(1)}, f32[8,128,128]{2,1,0:T(8,128)}, u32[]{:S(2)}, u32[]{:S(2)}) collective-permute-start(f32[8,128,128]{2,1,0:T(8,128)S(1)} %fusion.40), channel_id=1, source_target_pairs={{0,8},{4,12},{8,0},{12,4},{16,24},{20,28},{24,16},{28,20},{1,9},{5... | collective-permute-start | bytes 1572872 | tf_op jit(solution)/shard_map/ppermute | solution.py:37
  93.8 3.6 %collective-permute-start.20 = (f32[1,64,128]{2,1,0:T(8,128)S(1)}, f32[1,64,128]{2,1,0:T(8,128)}, u32[]{:S(2)}, u32[]{:S(2)}) collective-permute-start(f32[1,64,128]{2,1,0:T(8,128)S(1)} %broadcast.111), channel_id=1, source_target_pairs={{0,1},{1,2},{2,3},{4,5},{5,6},{6,7},{8,9},{9,10},{10,11},{12,13},{... | collective-permute-start | bytes 98312 | tf_op jit(solution)/shard_map/ppermute | solution.py:22
  98.1 4.2 %collective-permute-start.18 = (f32[4,64,128]{2,1,0:T(8,128)}, f32[4,64,128]{2,1,0:T(8,128)}, u32[]{:S(2)}, u32[]{:S(2)}) collective-permute-start(f32[4,64,128]{2,1,0:T(8,128)} %broadcast_in_dim.15), channel_id=1, source_target_pairs={{0,16},{4,20},{8,24},{12,28},{1,17},{5,21},{9,25},{13,29},{2,18},{... | collective-permute-start | bytes 393224 | tf_op jit(solution)/shard_map/ppermute | solution.py:31
  109.9 1.9 add.335
  111.8 1.9 slice.528
  115.5 1.9 slice.530
  117.4 1.8 slice.531
  122.1 3.0 %collective-permute-start.23 = (f32[1,64,128]{2,1,0:T(8,128)S(1)}, f32[1,64,128]{2,1,0:T(8,128)S(1)}, u32[]{:S(2)}, u32[]{:S(2)}) collective-permute-start(f32[1,64,128]{2,1,0:T(8,128)S(1)} %get-tuple-element.31), channel_id=1, source_target_pairs={{0,1},{1,2},{2,3},{4,5},{5,6},{6,7},{8,9},{9,10},{10,11},{12,13},{... | collective-permute-start | bytes 98312 | tf_op jit(solution)/shard_map/ppermute | solution.py:22
  126.6 3.4 %collective-permute-done.21 = f32[4,64,128]{2,1,0:T(8,128)S(1)} collective-permute-done((f32[4,64,128]{2,1,0:T(8,128)S(1)}, f32[4,64,128]{2,1,0:T(8,128)S(1)}, u32[]{:S(2)}, u32[]{:S(2)}) %collective-permute-start.21) | collective-permute-done | bytes 131104 | tf_op jit(solution)/shard_map/ppermute | solution.py:31
  131.5 3.0 %collective-permute-start.26 = (f32[1,64,128]{2,1,0:T(8,128)S(1)}, f32[1,64,128]{2,1,0:T(8,128)S(1)}, u32[]{:S(2)}, u32[]{:S(2)}) collective-permute-start(f32[1,64,128]{2,1,0:T(8,128)S(1)} %get-tuple-element.29), channel_id=1, source_target_pairs={{0,1},{1,2},{2,3},{4,5},{5,6},{6,7},{8,9},{9,10},{10,11},{12,13},{... | collective-permute-start | bytes 98312 | tf_op jit(solution)/shard_map/ppermute | solution.py:22
  134.6 5.3 %collective-permute-start.24 = (f32[4,64,128]{2,1,0:T(8,128)S(1)}, f32[4,64,128]{2,1,0:T(8,128)S(1)}, u32[]{:S(2)}, u32[]{:S(2)}) collective-permute-start(f32[4,64,128]{2,1,0:T(8,128)S(1)} %fusion.124), channel_id=1, source_target_pairs={{0,16},{4,20},{8,24},{12,28},{1,17},{5,21},{9,25},{13,29},{2,18},{... | collective-permute-start | bytes 393224 | tf_op jit(solution)/shard_map/ppermute | solution.py:31
  140.1 3.6 %collective-permute-done.24 = f32[4,64,128]{2,1,0:T(8,128)S(1)} collective-permute-done((f32[4,64,128]{2,1,0:T(8,128)S(1)}, f32[4,64,128]{2,1,0:T(8,128)S(1)}, u32[]{:S(2)}, u32[]{:S(2)}) %collective-permute-start.24) | collective-permute-done | bytes 131104 | tf_op jit(solution)/shard_map/ppermute | solution.py:31
  145.3 3.0 %collective-permute-start.29 = (f32[1,64,128]{2,1,0:T(8,128)S(1)}, f32[1,64,128]{2,1,0:T(8,128)S(1)}, u32[]{:S(2)}, u32[]{:S(2)}) collective-permute-start(f32[1,64,128]{2,1,0:T(8,128)S(1)} %get-tuple-element.27), channel_id=1, source_target_pairs={{0,1},{1,2},{2,3},{4,5},{5,6},{6,7},{8,9},{9,10},{10,11},{12,13},{... | collective-permute-start | bytes 98312 | tf_op jit(solution)/shard_map/ppermute | solution.py:22
  148.3 5.3 %collective-permute-start.27 = (f32[4,64,128]{2,1,0:T(8,128)S(1)}, f32[4,64,128]{2,1,0:T(8,128)S(1)}, u32[]{:S(2)}, u32[]{:S(2)}) collective-permute-start(f32[4,64,128]{2,1,0:T(8,128)S(1)} %fusion.135), channel_id=1, source_target_pairs={{0,16},{4,20},{8,24},{12,28},{1,17},{5,21},{9,25},{13,29},{2,18},{... | collective-permute-start | bytes 393224 | tf_op jit(solution)/shard_map/ppermute | solution.py:31
  153.8 3.3 %collective-permute-done.27 = f32[4,64,128]{2,1,0:T(8,128)S(1)} collective-permute-done((f32[4,64,128]{2,1,0:T(8,128)S(1)}, f32[4,64,128]{2,1,0:T(8,128)S(1)}, u32[]{:S(2)}, u32[]{:S(2)}) %collective-permute-start.27) | collective-permute-done | bytes 131104 | tf_op jit(solution)/shard_map/ppermute | solution.py:31
  157.6 6.5 %collective-permute-start.30 = (f32[8,128,128]{2,1,0:T(8,128)S(1)}, f32[8,128,128]{2,1,0:T(8,128)S(1)}, u32[]{:S(2)}, u32[]{:S(2)}) collective-permute-start(f32[8,128,128]{2,1,0:T(8,128)S(1)} %add.361), channel_id=1, source_target_pairs={{0,8},{4,12},{8,16},{12,20},{16,24},{20,28},{1,9},{5,13},{9,17},{1... | collective-permute-start | bytes 1572872 | tf_op jit(solution)/shard_map/ppermute | solution.py:31
  165.4 3.0 %collective-permute-start.32 = (f32[1,128,128]{2,1,0:T(8,128)S(1)}, f32[1,128,128]{2,1,0:T(8,128)S(1)}, u32[]{:S(2)}, u32[]{:S(2)}) collective-permute-start(f32[1,128,128]{2,1,0:T(8,128)S(1)} %get-tuple-element.17), channel_id=1, source_target_pairs={{0,1},{1,2},{2,3},{4,5},{5,6},{6,7},{8,9},{9,10},{10,11},{12,13},{... | collective-permute-start | bytes 196616 | tf_op jit(solution)/shard_map/ppermute | solution.py:22
  169.8 5.9 %collective-permute-done.30 = f32[8,128,128]{2,1,0:T(8,128)S(1)} collective-permute-done((f32[8,128,128]{2,1,0:T(8,128)S(1)}, f32[8,128,128]{2,1,0:T(8,128)S(1)}, u32[]{:S(2)}, u32[]{:S(2)}) %collective-permute-start.30) | collective-permute-done | bytes 524320 | tf_op jit(solution)/shard_map/ppermute | solution.py:31
  176.3 4.4 %collective-permute-start.33 = (f32[8,128,128]{2,1,0:T(8,128)S(1)}, f32[8,128,128]{2,1,0:T(8,128)S(1)}, u32[]{:S(2)}, u32[]{:S(2)}) collective-permute-start(f32[8,128,128]{2,1,0:T(8,128)S(1)} %fusion.50), channel_id=1, source_target_pairs={{0,8},{4,12},{8,16},{12,20},{16,24},{20,28},{1,9},{5,13},{9,17},{1... | collective-permute-start | bytes 1572872 | tf_op jit(solution)/shard_map/ppermute | solution.py:31
  182.0 3.2 %collective-permute-start.35 = (f32[1,128,128]{2,1,0:T(8,128)S(1)}, f32[1,128,128]{2,1,0:T(8,128)S(1)}, u32[]{:S(2)}, u32[]{:S(2)}) collective-permute-start(f32[1,128,128]{2,1,0:T(8,128)S(1)} %get-tuple-element.15), channel_id=1, source_target_pairs={{0,1},{1,2},{2,3},{4,5},{5,6},{6,7},{8,9},{9,10},{10,11},{12,13},{... | collective-permute-start | bytes 196616 | tf_op jit(solution)/shard_map/ppermute | solution.py:22
  186.5 5.0 %collective-permute-done.33 = f32[8,128,128]{2,1,0:T(8,128)S(1)} collective-permute-done((f32[8,128,128]{2,1,0:T(8,128)S(1)}, f32[8,128,128]{2,1,0:T(8,128)S(1)}, u32[]{:S(2)}, u32[]{:S(2)}) %collective-permute-start.33) | collective-permute-done | bytes 524320 | tf_op jit(solution)/shard_map/ppermute | solution.py:31
  192.1 3.4 %collective-permute-start.36 = (f32[8,128,128]{2,1,0:T(8,128)S(1)}, f32[8,128,128]{2,1,0:T(8,128)S(1)}, u32[]{:S(2)}, u32[]{:S(2)}) collective-permute-start(f32[8,128,128]{2,1,0:T(8,128)S(1)} %fusion.61), channel_id=1, source_target_pairs={{0,4},{4,8},{8,12},{12,16},{16,20},{20,24},{24,28},{1,5},{5,9},{9,... | collective-permute-start | bytes 1572872 | tf_op jit(solution)/shard_map/ppermute | solution.py:31
  196.9 3.0 %collective-permute-start.38 = (f32[1,128,128]{2,1,0:T(8,128)S(1)}, f32[1,128,128]{2,1,0:T(8,128)S(1)}, u32[]{:S(2)}, u32[]{:S(2)}) collective-permute-start(f32[1,128,128]{2,1,0:T(8,128)S(1)} %get-tuple-element.13), channel_id=1, source_target_pairs={{0,1},{1,2},{2,3},{4,5},{5,6},{6,7},{8,9},{9,10},{10,11},{12,13},{... | collective-permute-start | bytes 196616 | tf_op jit(solution)/shard_map/ppermute | solution.py:22
  201.3 4.2 %collective-permute-done.36 = f32[8,128,128]{2,1,0:T(8,128)S(1)} collective-permute-done((f32[8,128,128]{2,1,0:T(8,128)S(1)}, f32[8,128,128]{2,1,0:T(8,128)S(1)}, u32[]{:S(2)}, u32[]{:S(2)}) %collective-permute-start.36) | collective-permute-done | bytes 524320 | tf_op jit(solution)/shard_map/ppermute | solution.py:31
  206.1 4.4 %collective-permute-start.39 = (f32[8,128,128]{2,1,0:T(8,128)S(1)}, f32[8,128,128]{2,1,0:T(8,128)S(1)}, u32[]{:S(2)}, u32[]{:S(2)}) collective-permute-start(f32[8,128,128]{2,1,0:T(8,128)S(1)} %fusion.71), channel_id=1, source_target_pairs={{0,4},{4,8},{8,12},{12,16},{16,20},{20,24},{24,28},{1,5},{5,9},{9,... | collective-permute-start | bytes 1572872 | tf_op jit(solution)/shard_map/ppermute | solution.py:31
  211.8 3.0 %collective-permute-start.41 = (f32[1,128,128]{2,1,0:T(8,128)S(1)}, f32[1,128,128]{2,1,0:T(8,128)S(1)}, u32[]{:S(2)}, u32[]{:S(2)}) collective-permute-start(f32[1,128,128]{2,1,0:T(8,128)S(1)} %get-tuple-element.11), channel_id=1, source_target_pairs={{0,1},{1,2},{2,3},{4,5},{5,6},{6,7},{8,9},{9,10},{10,11},{12,13},{... | collective-permute-start | bytes 196616 | tf_op jit(solution)/shard_map/ppermute | solution.py:22
  216.2 3.3 %collective-permute-done.39 = f32[8,128,128]{2,1,0:T(8,128)S(1)} collective-permute-done((f32[8,128,128]{2,1,0:T(8,128)S(1)}, f32[8,128,128]{2,1,0:T(8,128)S(1)}, u32[]{:S(2)}, u32[]{:S(2)}) %collective-permute-start.39) | collective-permute-done | bytes 524320 | tf_op jit(solution)/shard_map/ppermute | solution.py:31
  220.2 5.3 %collective-permute-start.42 = (f32[8,128,128]{2,1,0:T(8,128)S(1)}, f32[8,128,128]{2,1,0:T(8,128)S(1)}, u32[]{:S(2)}, u32[]{:S(2)}) collective-permute-start(f32[8,128,128]{2,1,0:T(8,128)S(1)} %fusion.81), channel_id=1, source_target_pairs={{0,4},{4,8},{8,12},{12,16},{16,20},{20,24},{24,28},{1,5},{5,9},{9,... | collective-permute-start | bytes 1572872 | tf_op jit(solution)/shard_map/ppermute | solution.py:31
  226.9 3.0 %collective-permute-start.44 = (f32[1,128,128]{2,1,0:T(8,128)S(1)}, f32[1,128,128]{2,1,0:T(8,128)S(1)}, u32[]{:S(2)}, u32[]{:S(2)}) collective-permute-start(f32[1,128,128]{2,1,0:T(8,128)S(1)} %get-tuple-element.9), channel_id=1, source_target_pairs={{0,1},{1,2},{2,3},{4,5},{5,6},{6,7},{8,9},{9,10},{10,11},{12,13},{... | collective-permute-start | bytes 196616 | tf_op jit(solution)/shard_map/ppermute | solution.py:22
  231.3 2.7 %collective-permute-done.42 = f32[8,128,128]{2,1,0:T(8,128)S(1)} collective-permute-done((f32[8,128,128]{2,1,0:T(8,128)S(1)}, f32[8,128,128]{2,1,0:T(8,128)S(1)}, u32[]{:S(2)}, u32[]{:S(2)}) %collective-permute-start.42) | collective-permute-done | bytes 524320 | tf_op jit(solution)/shard_map/ppermute | solution.py:31
  (121 shorter events, 53.3 us)
Async XLA Ops:
  0.7 16.1 %collective-permute-start = (f32[8,128,128]{2,1,0:T(8,128)S(1)}, f32[8,128,128]{2,1,0:T(8,128)S(1)}, u32[]{:S(2)}, u32[]{:S(2)}) collective-permute-start(f32[8,128,128]{2,1,0:T(8,128)S(1)} %slice.484), channel_id=1, source_target_pairs={{0,4},{4,8},{8,12},{12,16},{16,20},{20,24},{24,28},{1,5},{5,9},{9,... | collective-permute-start | bytes 1572872 | tf_op jit(solution)/shard_map/ppermute | solution.py:31
  5.6 4.3 %collective-permute-start.1 = (f32[1,128,128]{2,1,0:T(8,128)S(1)}, f32[1,128,128]{2,1,0:T(8,128)S(1)}, u32[]{:S(2)}, u32[]{:S(2)}) collective-permute-start(f32[1,128,128]{2,1,0:T(8,128)S(1)} %broadcast.105), channel_id=1, source_target_pairs={{1,0},{2,1},{3,2},{5,4},{6,5},{7,6},{9,8},{10,9},{11,10},{13,12},{... | collective-permute-start | bytes 196616 | tf_op jit(solution)/shard_map/ppermute | solution.py:23
  6.9 3.9 %collective-permute-start.2 = (f32[1,128,128]{2,1,0:T(8,128)S(1)}, f32[1,128,128]{2,1,0:T(8,128)S(1)}, u32[]{:S(2)}, u32[]{:S(2)}) collective-permute-start(f32[1,128,128]{2,1,0:T(8,128)S(1)} %broadcast.105), channel_id=1, source_target_pairs={{0,1},{1,2},{2,3},{4,5},{5,6},{6,7},{8,9},{9,10},{10,11},{12,13},{... | collective-permute-start | bytes 196616 | tf_op jit(solution)/shard_map/ppermute | solution.py:22
  11.3 5.5 %copy-start = (f32[8,128,128]{2,1,0:T(8,128)S(1)}, f32[8,128,128]{2,1,0:T(8,128)}, u32[]{:S(2)}) copy-start(f32[8,128,128]{2,1,0:T(8,128)} %param.3) | copy-start | bytes 1572868
  11.3 5.5 %copy-start.1 = (f32[1,8,128,128]{3,2,1,0:T(8,128)S(1)}, f32[1,8,128,128]{3,2,1,0:T(8,128)}, u32[]{:S(2)}) copy-start(f32[1,8,128,128]{3,2,1,0:T(8,128)} %param.2) | copy-start | bytes 1572868
  17.3 14.7 %collective-permute-start.3 = (f32[8,128,128]{2,1,0:T(8,128)S(1)}, f32[8,128,128]{2,1,0:T(8,128)S(1)}, u32[]{:S(2)}, u32[]{:S(2)}) collective-permute-start(f32[8,128,128]{2,1,0:T(8,128)S(1)} %get-tuple-element.7), channel_id=1, source_target_pairs={{0,4},{4,8},{8,12},{12,16},{16,20},{20,24},{24,28},{1,5},{5,9},{9,... | collective-permute-start | bytes 1572872 | tf_op jit(solution)/shard_map/ppermute | solution.py:31
  21.8 4.3 %collective-permute-start.4 = (f32[1,128,128]{2,1,0:T(8,128)S(1)}, f32[1,128,128]{2,1,0:T(8,128)S(1)}, u32[]{:S(2)}, u32[]{:S(2)}) collective-permute-start(f32[1,128,128]{2,1,0:T(8,128)S(1)} %get-tuple-element.26), channel_id=1, source_target_pairs={{1,0},{2,1},{3,2},{5,4},{6,5},{7,6},{9,8},{10,9},{11,10},{13,12},{... | collective-permute-start | bytes 196616 | tf_op jit(solution)/shard_map/ppermute | solution.py:23
  23.1 3.9 %collective-permute-start.5 = (f32[1,128,128]{2,1,0:T(8,128)S(1)}, f32[1,128,128]{2,1,0:T(8,128)S(1)}, u32[]{:S(2)}, u32[]{:S(2)}) collective-permute-start(f32[1,128,128]{2,1,0:T(8,128)S(1)} %get-tuple-element.25), channel_id=1, source_target_pairs={{0,1},{1,2},{2,3},{4,5},{5,6},{6,7},{8,9},{9,10},{10,11},{12,13},{... | collective-permute-start | bytes 196616 | tf_op jit(solution)/shard_map/ppermute | solution.py:22
  32.7 13.8 %collective-permute-start.6 = (f32[8,128,128]{2,1,0:T(8,128)S(1)}, f32[8,128,128]{2,1,0:T(8,128)S(1)}, u32[]{:S(2)}, u32[]{:S(2)}) collective-permute-start(f32[8,128,128]{2,1,0:T(8,128)S(1)} %fusion.16), channel_id=1, source_target_pairs={{0,4},{4,8},{8,12},{12,16},{16,20},{20,24},{24,28},{1,5},{5,9},{9,... | collective-permute-start | bytes 1572872 | tf_op jit(solution)/shard_map/ppermute | solution.py:31
  37.1 8.1 %collective-permute-start.7 = (f32[1,128,128]{2,1,0:T(8,128)S(1)}, f32[1,128,128]{2,1,0:T(8,128)S(1)}, u32[]{:S(2)}, u32[]{:S(2)}) collective-permute-start(f32[1,128,128]{2,1,0:T(8,128)S(1)} %get-tuple-element.24), channel_id=1, source_target_pairs={{1,0},{2,1},{3,2},{5,4},{6,5},{7,6},{9,8},{10,9},{11,10},{13,12},{... | collective-permute-start | bytes 196616 | tf_op jit(solution)/shard_map/ppermute | solution.py:23
  38.4 6.8 %collective-permute-start.8 = (f32[1,128,128]{2,1,0:T(8,128)S(1)}, f32[1,128,128]{2,1,0:T(8,128)S(1)}, u32[]{:S(2)}, u32[]{:S(2)}) collective-permute-start(f32[1,128,128]{2,1,0:T(8,128)S(1)} %get-tuple-element.23), channel_id=1, source_target_pairs={{0,1},{1,2},{2,3},{4,5},{5,6},{6,7},{8,9},{9,10},{10,11},{12,13},{... | collective-permute-start | bytes 196616 | tf_op jit(solution)/shard_map/ppermute | solution.py:22
  41.4 15.9 %collective-permute-start.10 = (f32[8,128,128]{2,1,0:T(8,128)S(1)}, f32[8,128,128]{2,1,0:T(8,128)S(1)}, u32[]{:S(2)}, u32[]{:S(2)}) collective-permute-start(f32[8,128,128]{2,1,0:T(8,128)S(1)} %slice.484), channel_id=1, source_target_pairs={{0,8},{4,12},{8,16},{12,20},{16,24},{20,28},{1,9},{5,13},{9,17},{1... | collective-permute-start | bytes 1572872 | tf_op jit(solution)/shard_map/ppermute | solution.py:31
  47.2 15.3 %collective-permute-start.9 = (f32[8,128,128]{2,1,0:T(8,128)S(1)}, f32[8,128,128]{2,1,0:T(8,128)S(1)}, u32[]{:S(2)}, u32[]{:S(2)}) collective-permute-start(f32[8,128,128]{2,1,0:T(8,128)S(1)} %fusion.23), channel_id=1, source_target_pairs={{0,4},{4,0},{8,12},{12,8},{16,20},{20,16},{24,28},{28,24},{1,5},{5... | collective-permute-start | bytes 1572872 | tf_op jit(solution)/shard_map/ppermute | solution.py:37
  62.7 12.2 %collective-permute-start.11 = (f32[8,128,128]{2,1,0:T(8,128)S(1)}, f32[8,128,128]{2,1,0:T(8,128)S(1)}, u32[]{:S(2)}, u32[]{:S(2)}) collective-permute-start(f32[8,128,128]{2,1,0:T(8,128)S(1)} %get-tuple-element.5), channel_id=1, source_target_pairs={{0,8},{4,12},{8,16},{12,20},{16,24},{20,28},{1,9},{5,13},{9,17},{1... | collective-permute-start | bytes 1572872 | tf_op jit(solution)/shard_map/ppermute | solution.py:31
  66.2 4.3 %collective-permute-start.12 = (f32[1,128,128]{2,1,0:T(8,128)S(1)}, f32[1,128,128]{2,1,0:T(8,128)S(1)}, u32[]{:S(2)}, u32[]{:S(2)}) collective-permute-start(f32[1,128,128]{2,1,0:T(8,128)S(1)} %get-tuple-element.22), channel_id=1, source_target_pairs={{1,0},{2,1},{3,2},{5,4},{6,5},{7,6},{9,8},{10,9},{11,10},{13,12},{... | collective-permute-start | bytes 196616 | tf_op jit(solution)/shard_map/ppermute | solution.py:23
  67.5 3.9 %collective-permute-start.13 = (f32[1,128,128]{2,1,0:T(8,128)S(1)}, f32[1,128,128]{2,1,0:T(8,128)S(1)}, u32[]{:S(2)}, u32[]{:S(2)}) collective-permute-start(f32[1,128,128]{2,1,0:T(8,128)S(1)} %get-tuple-element.21), channel_id=1, source_target_pairs={{0,1},{1,2},{2,3},{4,5},{5,6},{6,7},{8,9},{9,10},{10,11},{12,13},{... | collective-permute-start | bytes 196616 | tf_op jit(solution)/shard_map/ppermute | solution.py:22
  75.5 13.7 %collective-permute-start.14 = (f32[8,128,128]{2,1,0:T(8,128)S(1)}, f32[8,128,128]{2,1,0:T(8,128)S(1)}, u32[]{:S(2)}, u32[]{:S(2)}) collective-permute-start(f32[8,128,128]{2,1,0:T(8,128)S(1)} %fusion.33), channel_id=1, source_target_pairs={{0,8},{4,12},{8,16},{12,20},{16,24},{20,28},{1,9},{5,13},{9,17},{1... | collective-permute-start | bytes 1572872 | tf_op jit(solution)/shard_map/ppermute | solution.py:31
  80.0 4.3 %collective-permute-start.15 = (f32[1,128,128]{2,1,0:T(8,128)S(1)}, f32[1,128,128]{2,1,0:T(8,128)S(1)}, u32[]{:S(2)}, u32[]{:S(2)}) collective-permute-start(f32[1,128,128]{2,1,0:T(8,128)S(1)} %get-tuple-element.20), channel_id=1, source_target_pairs={{1,0},{2,1},{3,2},{5,4},{6,5},{7,6},{9,8},{10,9},{11,10},{13,12},{... | collective-permute-start | bytes 196616 | tf_op jit(solution)/shard_map/ppermute | solution.py:23
  81.3 3.9 %collective-permute-start.16 = (f32[1,128,128]{2,1,0:T(8,128)S(1)}, f32[1,128,128]{2,1,0:T(8,128)S(1)}, u32[]{:S(2)}, u32[]{:S(2)}) collective-permute-start(f32[1,128,128]{2,1,0:T(8,128)S(1)} %get-tuple-element.19), channel_id=1, source_target_pairs={{0,1},{1,2},{2,3},{4,5},{5,6},{6,7},{8,9},{9,10},{10,11},{12,13},{... | collective-permute-start | bytes 196616 | tf_op jit(solution)/shard_map/ppermute | solution.py:22
  90.0 20.0 %collective-permute-start.17 = (f32[8,128,128]{2,1,0:T(8,128)S(1)}, f32[8,128,128]{2,1,0:T(8,128)}, u32[]{:S(2)}, u32[]{:S(2)}) collective-permute-start(f32[8,128,128]{2,1,0:T(8,128)S(1)} %fusion.40), channel_id=1, source_target_pairs={{0,8},{4,12},{8,0},{12,4},{16,24},{20,28},{24,16},{28,20},{1,9},{5... | collective-permute-start | bytes 1572872 | tf_op jit(solution)/shard_map/ppermute | solution.py:37
  92.5 15.0 %collective-permute-start.19 = (f32[1,64,128]{2,1,0:T(8,128)S(1)}, f32[1,64,128]{2,1,0:T(8,128)S(1)}, u32[]{:S(2)}, u32[]{:S(2)}) collective-permute-start(f32[1,64,128]{2,1,0:T(8,128)S(1)} %broadcast.111), channel_id=1, source_target_pairs={{1,0},{2,1},{3,2},{5,4},{6,5},{7,6},{9,8},{10,9},{11,10},{13,12},{... | collective-permute-start | bytes 98312 | tf_op jit(solution)/shard_map/ppermute | solution.py:23
  93.8 14.3 %collective-permute-start.20 = (f32[1,64,128]{2,1,0:T(8,128)S(1)}, f32[1,64,128]{2,1,0:T(8,128)}, u32[]{:S(2)}, u32[]{:S(2)}) collective-permute-start(f32[1,64,128]{2,1,0:T(8,128)S(1)} %broadcast.111), channel_id=1, source_target_pairs={{0,1},{1,2},{2,3},{4,5},{5,6},{6,7},{8,9},{9,10},{10,11},{12,13},{... | collective-permute-start | bytes 98312 | tf_op jit(solution)/shard_map/ppermute | solution.py:22
  98.1 21.2 %collective-permute-start.18 = (f32[4,64,128]{2,1,0:T(8,128)}, f32[4,64,128]{2,1,0:T(8,128)}, u32[]{:S(2)}, u32[]{:S(2)}) collective-permute-start(f32[4,64,128]{2,1,0:T(8,128)} %broadcast_in_dim.15), channel_id=1, source_target_pairs={{0,16},{4,20},{8,24},{12,28},{1,17},{5,21},{9,25},{13,29},{2,18},{... | collective-permute-start | bytes 393224 | tf_op jit(solution)/shard_map/ppermute | solution.py:31
  120.8 5.6 %collective-permute-start.22 = (f32[1,64,128]{2,1,0:T(8,128)S(1)}, f32[1,64,128]{2,1,0:T(8,128)S(1)}, u32[]{:S(2)}, u32[]{:S(2)}) collective-permute-start(f32[1,64,128]{2,1,0:T(8,128)S(1)} %get-tuple-element.32), channel_id=1, source_target_pairs={{1,0},{2,1},{3,2},{5,4},{6,5},{7,6},{9,8},{10,9},{11,10},{13,12},{... | collective-permute-start | bytes 98312 | tf_op jit(solution)/shard_map/ppermute | solution.py:23
  122.1 4.4 %collective-permute-start.23 = (f32[1,64,128]{2,1,0:T(8,128)S(1)}, f32[1,64,128]{2,1,0:T(8,128)S(1)}, u32[]{:S(2)}, u32[]{:S(2)}) collective-permute-start(f32[1,64,128]{2,1,0:T(8,128)S(1)} %get-tuple-element.31), channel_id=1, source_target_pairs={{0,1},{1,2},{2,3},{4,5},{5,6},{6,7},{8,9},{9,10},{10,11},{12,13},{... | collective-permute-start | bytes 98312 | tf_op jit(solution)/shard_map/ppermute | solution.py:22
  125.1 4.9 %collective-permute-start.21 = (f32[4,64,128]{2,1,0:T(8,128)S(1)}, f32[4,64,128]{2,1,0:T(8,128)S(1)}, u32[]{:S(2)}, u32[]{:S(2)}) collective-permute-start(f32[4,64,128]{2,1,0:T(8,128)S(1)} %get-tuple-element.2), channel_id=1, source_target_pairs={{0,16},{4,20},{8,24},{12,28},{1,17},{5,21},{9,25},{13,29},{2,18},{... | collective-permute-start | bytes 393224 | tf_op jit(solution)/shard_map/ppermute | solution.py:31
  130.2 9.7 %collective-permute-start.25 = (f32[1,64,128]{2,1,0:T(8,128)S(1)}, f32[1,64,128]{2,1,0:T(8,128)S(1)}, u32[]{:S(2)}, u32[]{:S(2)}) collective-permute-start(f32[1,64,128]{2,1,0:T(8,128)S(1)} %get-tuple-element.30), channel_id=1, source_target_pairs={{1,0},{2,1},{3,2},{5,4},{6,5},{7,6},{9,8},{10,9},{11,10},{13,12},{... | collective-permute-start | bytes 98312 | tf_op jit(solution)/shard_map/ppermute | solution.py:23
  131.5 8.4 %collective-permute-start.26 = (f32[1,64,128]{2,1,0:T(8,128)S(1)}, f32[1,64,128]{2,1,0:T(8,128)S(1)}, u32[]{:S(2)}, u32[]{:S(2)}) collective-permute-start(f32[1,64,128]{2,1,0:T(8,128)S(1)} %get-tuple-element.29), channel_id=1, source_target_pairs={{0,1},{1,2},{2,3},{4,5},{5,6},{6,7},{8,9},{9,10},{10,11},{12,13},{... | collective-permute-start | bytes 98312 | tf_op jit(solution)/shard_map/ppermute | solution.py:22
  134.6 9.2 %collective-permute-start.24 = (f32[4,64,128]{2,1,0:T(8,128)S(1)}, f32[4,64,128]{2,1,0:T(8,128)S(1)}, u32[]{:S(2)}, u32[]{:S(2)}) collective-permute-start(f32[4,64,128]{2,1,0:T(8,128)S(1)} %fusion.124), channel_id=1, source_target_pairs={{0,16},{4,20},{8,24},{12,28},{1,17},{5,21},{9,25},{13,29},{2,18},{... | collective-permute-start | bytes 393224 | tf_op jit(solution)/shard_map/ppermute | solution.py:31
  144.0 9.6 %collective-permute-start.28 = (f32[1,64,128]{2,1,0:T(8,128)S(1)}, f32[1,64,128]{2,1,0:T(8,128)S(1)}, u32[]{:S(2)}, u32[]{:S(2)}) collective-permute-start(f32[1,64,128]{2,1,0:T(8,128)S(1)} %get-tuple-element.28), channel_id=1, source_target_pairs={{1,0},{2,1},{3,2},{5,4},{6,5},{7,6},{9,8},{10,9},{11,10},{13,12},{... | collective-permute-start | bytes 98312 | tf_op jit(solution)/shard_map/ppermute | solution.py:23
  145.3 8.4 %collective-permute-start.29 = (f32[1,64,128]{2,1,0:T(8,128)S(1)}, f32[1,64,128]{2,1,0:T(8,128)S(1)}, u32[]{:S(2)}, u32[]{:S(2)}) collective-permute-start(f32[1,64,128]{2,1,0:T(8,128)S(1)} %get-tuple-element.27), channel_id=1, source_target_pairs={{0,1},{1,2},{2,3},{4,5},{5,6},{6,7},{8,9},{9,10},{10,11},{12,13},{... | collective-permute-start | bytes 98312 | tf_op jit(solution)/shard_map/ppermute | solution.py:22
  148.3 8.8 %collective-permute-start.27 = (f32[4,64,128]{2,1,0:T(8,128)S(1)}, f32[4,64,128]{2,1,0:T(8,128)S(1)}, u32[]{:S(2)}, u32[]{:S(2)}) collective-permute-start(f32[4,64,128]{2,1,0:T(8,128)S(1)} %fusion.135), channel_id=1, source_target_pairs={{0,16},{4,20},{8,24},{12,28},{1,17},{5,21},{9,25},{13,29},{2,18},{... | collective-permute-start | bytes 393224 | tf_op jit(solution)/shard_map/ppermute | solution.py:31
  157.6 18.1 %collective-permute-start.30 = (f32[8,128,128]{2,1,0:T(8,128)S(1)}, f32[8,128,128]{2,1,0:T(8,128)S(1)}, u32[]{:S(2)}, u32[]{:S(2)}) collective-permute-start(f32[8,128,128]{2,1,0:T(8,128)S(1)} %add.361), channel_id=1, source_target_pairs={{0,8},{4,12},{8,16},{12,20},{16,24},{20,28},{1,9},{5,13},{9,17},{1... | collective-permute-start | bytes 1572872 | tf_op jit(solution)/shard_map/ppermute | solution.py:31
  164.1 4.3 %collective-permute-start.31 = (f32[1,128,128]{2,1,0:T(8,128)S(1)}, f32[1,128,128]{2,1,0:T(8,128)S(1)}, u32[]{:S(2)}, u32[]{:S(2)}) collective-permute-start(f32[1,128,128]{2,1,0:T(8,128)S(1)} %get-tuple-element.18), channel_id=1, source_target_pairs={{1,0},{2,1},{3,2},{5,4},{6,5},{7,6},{9,8},{10,9},{11,10},{13,12},{... | collective-permute-start | bytes 196616 | tf_op jit(solution)/shard_map/ppermute | solution.py:23
  165.4 3.9 %collective-permute-start.32 = (f32[1,128,128]{2,1,0:T(8,128)S(1)}, f32[1,128,128]{2,1,0:T(8,128)S(1)}, u32[]{:S(2)}, u32[]{:S(2)}) collective-permute-start(f32[1,128,128]{2,1,0:T(8,128)S(1)} %get-tuple-element.17), channel_id=1, source_target_pairs={{0,1},{1,2},{2,3},{4,5},{5,6},{6,7},{8,9},{9,10},{10,11},{12,13},{... | collective-permute-start | bytes 196616 | tf_op jit(solution)/shard_map/ppermute | solution.py:22
  176.3 15.2 %collective-permute-start.33 = (f32[8,128,128]{2,1,0:T(8,128)S(1)}, f32[8,128,128]{2,1,0:T(8,128)S(1)}, u32[]{:S(2)}, u32[]{:S(2)}) collective-permute-start(f32[8,128,128]{2,1,0:T(8,128)S(1)} %fusion.50), channel_id=1, source_target_pairs={{0,8},{4,12},{8,16},{12,20},{16,24},{20,28},{1,9},{5,13},{9,17},{1... | collective-permute-start | bytes 1572872 | tf_op jit(solution)/shard_map/ppermute | solution.py:31
  180.7 4.5 %collective-permute-start.34 = (f32[1,128,128]{2,1,0:T(8,128)S(1)}, f32[1,128,128]{2,1,0:T(8,128)S(1)}, u32[]{:S(2)}, u32[]{:S(2)}) collective-permute-start(f32[1,128,128]{2,1,0:T(8,128)S(1)} %get-tuple-element.16), channel_id=1, source_target_pairs={{1,0},{2,1},{3,2},{5,4},{6,5},{7,6},{9,8},{10,9},{11,10},{13,12},{... | collective-permute-start | bytes 196616 | tf_op jit(solution)/shard_map/ppermute | solution.py:23
  182.0 3.9 %collective-permute-start.35 = (f32[1,128,128]{2,1,0:T(8,128)S(1)}, f32[1,128,128]{2,1,0:T(8,128)S(1)}, u32[]{:S(2)}, u32[]{:S(2)}) collective-permute-start(f32[1,128,128]{2,1,0:T(8,128)S(1)} %get-tuple-element.15), channel_id=1, source_target_pairs={{0,1},{1,2},{2,3},{4,5},{5,6},{6,7},{8,9},{9,10},{10,11},{12,13},{... | collective-permute-start | bytes 196616 | tf_op jit(solution)/shard_map/ppermute | solution.py:22
  192.1 13.3 %collective-permute-start.36 = (f32[8,128,128]{2,1,0:T(8,128)S(1)}, f32[8,128,128]{2,1,0:T(8,128)S(1)}, u32[]{:S(2)}, u32[]{:S(2)}) collective-permute-start(f32[8,128,128]{2,1,0:T(8,128)S(1)} %fusion.61), channel_id=1, source_target_pairs={{0,4},{4,8},{8,12},{12,16},{16,20},{20,24},{24,28},{1,5},{5,9},{9,... | collective-permute-start | bytes 1572872 | tf_op jit(solution)/shard_map/ppermute | solution.py:31
  195.6 4.3 %collective-permute-start.37 = (f32[1,128,128]{2,1,0:T(8,128)S(1)}, f32[1,128,128]{2,1,0:T(8,128)S(1)}, u32[]{:S(2)}, u32[]{:S(2)}) collective-permute-start(f32[1,128,128]{2,1,0:T(8,128)S(1)} %get-tuple-element.14), channel_id=1, source_target_pairs={{1,0},{2,1},{3,2},{5,4},{6,5},{7,6},{9,8},{10,9},{11,10},{13,12},{... | collective-permute-start | bytes 196616 | tf_op jit(solution)/shard_map/ppermute | solution.py:23
  196.9 3.9 %collective-permute-start.38 = (f32[1,128,128]{2,1,0:T(8,128)S(1)}, f32[1,128,128]{2,1,0:T(8,128)S(1)}, u32[]{:S(2)}, u32[]{:S(2)}) collective-permute-start(f32[1,128,128]{2,1,0:T(8,128)S(1)} %get-tuple-element.13), channel_id=1, source_target_pairs={{0,1},{1,2},{2,3},{4,5},{5,6},{6,7},{8,9},{9,10},{10,11},{12,13},{... | collective-permute-start | bytes 196616 | tf_op jit(solution)/shard_map/ppermute | solution.py:22
  206.1 13.5 %collective-permute-start.39 = (f32[8,128,128]{2,1,0:T(8,128)S(1)}, f32[8,128,128]{2,1,0:T(8,128)S(1)}, u32[]{:S(2)}, u32[]{:S(2)}) collective-permute-start(f32[8,128,128]{2,1,0:T(8,128)S(1)} %fusion.71), channel_id=1, source_target_pairs={{0,4},{4,8},{8,12},{12,16},{16,20},{20,24},{24,28},{1,5},{5,9},{9,... | collective-permute-start | bytes 1572872 | tf_op jit(solution)/shard_map/ppermute | solution.py:31
  210.5 4.3 %collective-permute-start.40 = (f32[1,128,128]{2,1,0:T(8,128)S(1)}, f32[1,128,128]{2,1,0:T(8,128)S(1)}, u32[]{:S(2)}, u32[]{:S(2)}) collective-permute-start(f32[1,128,128]{2,1,0:T(8,128)S(1)} %get-tuple-element.12), channel_id=1, source_target_pairs={{1,0},{2,1},{3,2},{5,4},{6,5},{7,6},{9,8},{10,9},{11,10},{13,12},{... | collective-permute-start | bytes 196616 | tf_op jit(solution)/shard_map/ppermute | solution.py:23
  211.8 3.9 %collective-permute-start.41 = (f32[1,128,128]{2,1,0:T(8,128)S(1)}, f32[1,128,128]{2,1,0:T(8,128)S(1)}, u32[]{:S(2)}, u32[]{:S(2)}) collective-permute-start(f32[1,128,128]{2,1,0:T(8,128)S(1)} %get-tuple-element.11), channel_id=1, source_target_pairs={{0,1},{1,2},{2,3},{4,5},{5,6},{6,7},{8,9},{9,10},{10,11},{12,13},{... | collective-permute-start | bytes 196616 | tf_op jit(solution)/shard_map/ppermute | solution.py:22
  220.2 13.7 %copy-start.2 = (f32[8,128,128]{2,1,0:T(8,128)}, f32[8,128,128]{2,1,0:T(8,128)S(1)}, u32[]{:S(2)}) copy-start(f32[8,128,128]{2,1,0:T(8,128)S(1)} %fusion.81) | copy-start | bytes 1572868
  220.2 13.7 %collective-permute-start.42 = (f32[8,128,128]{2,1,0:T(8,128)S(1)}, f32[8,128,128]{2,1,0:T(8,128)S(1)}, u32[]{:S(2)}, u32[]{:S(2)}) collective-permute-start(f32[8,128,128]{2,1,0:T(8,128)S(1)} %fusion.81), channel_id=1, source_target_pairs={{0,4},{4,8},{8,12},{12,16},{16,20},{20,24},{24,28},{1,5},{5,9},{9,... | collective-permute-start | bytes 1572872 | tf_op jit(solution)/shard_map/ppermute | solution.py:31
  225.6 4.3 %collective-permute-start.43 = (f32[1,128,128]{2,1,0:T(8,128)S(1)}, f32[1,128,128]{2,1,0:T(8,128)S(1)}, u32[]{:S(2)}, u32[]{:S(2)}) collective-permute-start(f32[1,128,128]{2,1,0:T(8,128)S(1)} %get-tuple-element.10), channel_id=1, source_target_pairs={{1,0},{2,1},{3,2},{5,4},{6,5},{7,6},{9,8},{10,9},{11,10},{13,12},{... | collective-permute-start | bytes 196616 | tf_op jit(solution)/shard_map/ppermute | solution.py:23
  226.9 3.9 %collective-permute-start.44 = (f32[1,128,128]{2,1,0:T(8,128)S(1)}, f32[1,128,128]{2,1,0:T(8,128)S(1)}, u32[]{:S(2)}, u32[]{:S(2)}) collective-permute-start(f32[1,128,128]{2,1,0:T(8,128)S(1)} %get-tuple-element.9), channel_id=1, source_target_pairs={{0,1},{1,2},{2,3},{4,5},{5,6},{6,7},{8,9},{9,10},{10,11},{12,13},{... | collective-permute-start | bytes 196616 | tf_op jit(solution)/shard_map/ppermute | solution.py:22
  (1 other events, 0.6 us)
where the time goes:
time: 239 us; the launch traced here: 235 us
  starting transfers between devices  133 us (56%)
  waiting for transfers between devices  67.7 us (28%)
  other arithmetic  17.1 us (7%)
  local copies, waits for them, and re-layouts  15.8 us (7%)
    ppermute x15, starting transfers between devices, shifted(): return lax.ppermute(shard, axis, pairs)  65.6 us
    ppermute x15, waiting for transfers between devices, shifted(): return lax.ppermute(shard, axis, pairs)  54.9 us
    ppermute x14, starting transfers between devices, padded_2(): before = lax.ppermute(last, axis, up)  43.2 us
    ppermute x14, starting transfers between devices, padded_2(): after = lax.ppermute(first, axis, down)  18.1 us
    ppermute x14, waiting for transfers between devices, padded_2(): before = lax.ppermute(last, axis, up)  7.67 us
    ppermute x2, starting transfers between devices, swapped(): return lax.ppermute(value, axis, pairs)  6.32 us
    concatenate x14, other arithmetic, padded_2(): shard = jnp.concatenate([before, shard, after], axis=dim)  5.63 us
    ppermute x2, waiting for transfers between devices, swapped(): return lax.ppermute(value, axis, pairs)  5.09 us
  transfers between devices with their start and end apart: 45, of which 24 were waited for; matrix products, arithmetic and copies ran while one was open for 10% of the time, Pallas kernels for 0%

commit v1 on v0

--- a/solution.py
+++ b/solution.py
@@ -1,6 +1,10 @@
+import functools
+
 import jax
 import jax.numpy as jnp
 from jax import lax
+from jax.experimental import pallas as pl
+from jax.experimental.pallas import tpu as pltpu
 from jax.sharding import PartitionSpec as P
 
 NU = 2
@@ -158,9 +162,426 @@
     return (solution[None], final_defect[None])
 
 
+MESH = pl.DeviceIdType.MESH
+
+
+def snake(index):
+    return index + ((index // 2) % 2) * (1 - 2 * (index % 2))
+
+
+def scaled(weights, stretch):
+    return tuple(stretch * weight for weight in weights)
+
+
+def fits(steps, peers, slabs, planes, rows, lanes):
+    block = rows // peers
+    return (
+        steps == peers
+        and peers % 8 == 0
+        and peers & (peers - 1) == 0
+        and rows % peers == 0
+        and block % 8 == 0
+        and planes % 2 == 0
+        and lanes % 128 == 0
+        and peers <= 16
+        and slabs > 1
+    )
+
+
+def cycle_kernel(
+    peers,
+    slabs,
+    source,
+    source_far,
+    conduct,
+    out_solution,
+    out_defect,
+    rhs, rhs1, rhs2, scrap,
+    cond, cond2, gain0, gain1, gain2,
+    a1, a2, a3, a4, a5, fd,
+    m1, m2, m3, m4,
+    k1, k2, k3, k4,
+    halo_z, halo_x, halo_z2, halo_x2,
+    in_send, in_recv, own_sem,
+    h_send, h_recv,
+    out_send, out_recv, out_own,
+):
+    planes, rows, lanes = source.shape
+    block = rows // peers
+    half_planes, half_block = planes // 2, block // 2
+    me, slab = lax.axis_index("tm"), lax.axis_index("space")
+    mine = snake(me)
+    following, preceding = snake((mine + 1) % peers), snake((mine + peers - 1) % peers)
+    has_next, has_prev = mine < peers - 1, mine > 0
+    has_up, has_down = slab < slabs - 1, slab > 0
+
+    barrier = pltpu.get_barrier_semaphore()
+    for k in range(1, peers):
+        pl.semaphore_signal(
+            barrier, inc=1, device_id={"tm": me ^ k}, device_id_type=MESH
+        )
+
+    @pl.when(has_up)
+    def _():
+        pl.semaphore_signal(barrier, inc=1, device_id={"space": slab + 1}, device_id_type=MESH)
+
+    @pl.when(has_down)
+    def _():
+        pl.semaphore_signal(barrier, inc=1, device_id={"space": slab - 1}, device_id_type=MESH)
+
+    neighbours = jnp.where(has_up, 1, 0) + jnp.where(has_down, 1, 0)
+    pl.semaphore_wait(barrier, peers - 1 + neighbours)
+
+    def rows_of(index):
+        return pl.ds(pl.multiple_of(snake(index) * block, 8), block)
+
+    def inward(peer, step, recv):
+        return pltpu.make_async_remote_copy(
+            src_ref=source.at[:, rows_of(peer), :],
+            dst_ref=rhs.at[:, :, step, :],
+            send_sem=in_send.at[peer],
+            recv_sem=in_recv.at[recv],
+            device_id={"tm": peer},
+            device_id_type=MESH,
+        )
+
+    order = sorted(range(1, peers), reverse=True)
+    for k in order:
+        inward(me ^ k, me, me).start()
+    own = pltpu.make_async_copy(
+        source_far.at[:, rows_of(me), :], rhs.at[:, :, me, :], own_sem
+    )
+    own.start()
+
+    def fill(z, _):
+        for x in range(block):
+            row = conduct[z, pl.ds(mine * block + x, 1), :]
+            value = jnp.broadcast_to(row, (peers, lanes))
+            cond[z, x] = value
+            gain0[z, x] = OMEGA / (1.0 + value * (2.0 * sum(FINE)))
+            gain1[z, x] = OMEGA / (1.0 + value * (4.0 * sum(FINE)))
+        return 0
+
+    lax.fori_loop(0, planes, fill, 0)
+
+    def fill2(z, _):
+        for x in range(half_block):
+            value = 0.25 * (
+                (cond[2 * z, 2 * x] + cond[2 * z + 1, 2 * x])
+                + (cond[2 * z, 2 * x + 1] + cond[2 * z + 1, 2 * x + 1])
+            )
+            cond2[z, x] = value
+            gain2[z, x] = OMEGA / (1.0 + value * (8.0 * sum(COARSE)))
+        return 0
+
+    lax.fori_loop(0, half_planes, fill2, 0)
+    for ref in (a1, a2, a3, a4, a5, m1, m2, m3, m4, k1, k2, k3):
+        depth, width = ref.shape[0], ref.shape[1]
+        face = jnp.zeros((width, peers, lanes), jnp.float32)
+        ref[0] = face
+        ref[depth - 1] = face
+        cell = jnp.zeros((peers, lanes), jnp.float32)
+
+        def edge(z, _):
+            ref[z, 0] = cell
+            ref[z, width - 1] = cell
+            return 0
+
+        lax.fori_loop(1, depth - 1, edge, 0)
+
+    time = lax.broadcasted_iota(jnp.int32, (1, peers, lanes), 1)
+    lane = lax.broadcasted_iota(jnp.int32, (1, peers, lanes), 2)
+    not_first, not_last = lane > 0, lane < lanes - 1
+
+    def prior(value, shift):
+        return jnp.where(time >= shift, pltpu.roll(value, shift, 1), 0.0)
+
+    def with_partner(value, shift):
+        even = (time // shift) % 2 == 0
+        return value + jnp.where(
+            even, pltpu.roll(value, peers - shift, 1), pltpu.roll(value, shift, 1)
+        )
+
+    def residual(ref, z, right, conductivity, weights, shift):
+        weight_z, weight_x, weight_y = weights
+        width = ref.shape[1] - 2
+        inner = slice(1, width + 1)
+        centre = ref[z + 1, inner]
+        along_z = ref[z, inner] + ref[z + 2, inner]
+        along_x = ref[z + 1, 0:width] + ref[z + 1, 2 : width + 2]
+        along_y = jnp.where(not_first, pltpu.roll(centre, 1, 2), 0.0) + jnp.where(
+            not_last, pltpu.roll(centre, lanes - 1, 2), 0.0
+        )
+        if weight_z == weight_x == weight_y:
+            around = weight_z * (6.0 * centre - (along_z + along_x + along_y))
+        else:
+            around = (2.0 * (weight_z + weight_x + weight_y)) * centre - (
+                weight_z * along_z + weight_x * along_x + weight_y * along_y
+            )
+        return centre, right + prior(centre, shift) - centre - conductivity * around
+
+    def sweep(new, old, right, conductivity, gain, weights, shift):
+        width = old.shape[1] - 2
+
+        def plane(z, _):
+            centre, left = residual(old, z, right[z], conductivity[z], weights, shift)
+            new[z + 1, 1 : width + 1] = centre + gain[z] * left
+            return 0
+
+        lax.fori_loop(0, old.shape[0] - 2, plane, 0)
+
+    def defect_into(new, off, old, right, conductivity, weights, shift):
+        width = old.shape[1] - 2
+
+        def plane(z, _):
+            new[z + off, off : width + off] = residual(
+                old, z, right[z], conductivity[z], weights, shift
+            )[1]
+            return 0
+
+        lax.fori_loop(0, old.shape[0] - 2, plane, 0)
+
+    def bufs(ref):
+        if ref.shape[0] == planes + 2:
+            return halo_z, halo_x
+        return halo_z2, halo_x2
+
+    def faces(ref, stage):
+        into_z, into_x = bufs(ref)
+        slot = stage_slot[stage]
+        depth, width = ref.shape[0] - 2, ref.shape[1] - 2
+        inner, deep = pl.ds(1, width), pl.ds(1, depth)
+
+        def copy(src, dst, side, device):
+            return pltpu.make_async_remote_copy(
+                src_ref=src,
+                dst_ref=dst,
+                send_sem=h_send.at[stage, side],
+                recv_sem=h_recv.at[stage, side],
+                device_id=device,
+                device_id_type=MESH,
+            )
+
+        return (
+            (has_up, has_down, copy(ref.at[depth, inner], into_z.at[slot, 0], 0, {"space": slab + 1})),
+            (has_down, has_up, copy(ref.at[1, inner], into_z.at[slot, 1], 1, {"space": slab - 1})),
+            (has_next, has_prev, copy(ref.at[deep, width], into_x.at[slot, 0], 2, {"tm": following})),
+            (has_prev, has_next, copy(ref.at[deep, 1], into_x.at[slot, 1], 3, {"tm": preceding})),
+        )
+
+    stage_slot = {0: 0, 1: 1, 2: 2, 3: 3, 4: 0, 5: 1, 6: 2, 7: 4, 8: 5, 9: 6, 10: 7, 11: 8}
+    sent = []
+
+    def send(ref, stage):
+        for sends, _, copy in faces(ref, stage):
+            pl.when(sends)(copy.start)
+        sent.append((ref, stage))
+
+    def receive(ref, stage, new, off, conductivity, gain, weights):
+        weight_z, weight_x, _ = weights
+        into_z, into_x = bufs(ref)
+        slot = stage_slot[stage]
+        depth, width = ref.shape[0] - 2, ref.shape[1] - 2
+        inner, deep = slice(off, off + width), slice(off, off + depth)
+        four = faces(ref, stage)
+
+        def scale(*index):
+            value = conductivity[index]
+            return value if gain is None else value * gain[index]
+
+        for side, z in ((0, 0), (1, depth - 1)):
+            _, arrives, copy = four[side]
+
+            @pl.when(arrives)
+            def _(copy=copy, side=side, z=z):
+                copy.wait_recv()
+                new[z + off, inner] += scale(z) * (weight_z * into_z[slot, side])
+
+        for side, x in ((0, 0), (1, width - 1)):
+            _, arrives, copy = four[side + 2]
+
+            @pl.when(arrives)
+            def _(copy=copy, side=side, x=x):
+                copy.wait_recv()
+                new[deep, x + off] += scale(slice(None), x) * (weight_x * into_x[slot, side])
+
+    fine, middle, coarse = FINE, scaled(FINE, 2.0), scaled(COARSE, 4.0)
+
+    own.wait()
+    for k in order:
+        inward(me, me ^ k, me ^ k).wait_recv()
+
+    def first(z, _):
+        a1[z + 1, 1 : block + 1] = gain0[z] * rhs[z]
+        return 0
+
+    lax.fori_loop(0, planes, first, 0)
+    send(a1, 0)
+    sweep(a2, a1, rhs, cond, gain0, fine, 1)
+    receive(a1, 0, a2, 1, cond, gain0, fine)
+    send(a2, 1)
+    defect_into(scrap, 0, a2, rhs, cond, fine, 1)
+    receive(a2, 1, scrap, 0, cond, None, fine)
+
+    def restrict_time(z, _):
+        value = with_partner(scrap[z], 1)
+        rhs1[z] = value
+        m1[z + 1, 1 : block + 1] = gain1[z] * value
+        return 0
+
+    lax.fori_loop(0, planes, restrict_time, 0)
+    send(m1, 2)
+    sweep(m2, m1, rhs1, cond, gain1, middle, 2)
+    receive(m1, 2, m2, 1, cond, gain1, middle)
+    send(m2, 3)
+    defect_into(scrap, 0, m2, rhs1, cond, middle, 2)
+    receive(m2, 3, scrap, 0, cond, None, middle)
+
+    def restrict(z, _):
+        for x in range(half_block):
+            quad = (scrap[2 * z, 2 * x] + scrap[2 * z + 1, 2 * x]) + (
+                scrap[2 * z, 2 * x + 1] + scrap[2 * z + 1, 2 * x + 1]
+            )
+            value = 0.25 * with_partner(quad[None], 2)[0]
+            rhs2[z, x] = value
+            k1[z + 1, x + 1] = gain2[z, x] * value
+        return 0
+
+    lax.fori_loop(0, half_planes, restrict, 0)
+    send(k1, 4)
+    sweep(k2, k1, rhs2, cond2, gain2, coarse, 4)
+    receive(k1, 4, k2, 1, cond2, gain2, coarse)
+    send(k2, 5)
+    sweep(k3, k2, rhs2, cond2, gain2, coarse, 4)
+    receive(k2, 5, k3, 1, cond2, gain2, coarse)
+    send(k3, 6)
+    sweep(k4, k3, rhs2, cond2, gain2, coarse, 4)
+    receive(k3, 6, k4, 1, cond2, gain2, coarse)
+
+    def prolong(z, _):
+        for x in range(half_block):
+            value = k4[z + 1, x + 1]
+            for dz in range(2):
+                for dx in range(2):
+                    at = (2 * z + dz + 1, 2 * x + dx + 1)
+                    m3[at] = m2[at] + value
+        return 0
+
+    lax.fori_loop(0, half_planes, prolong, 0)
+    send(m3, 7)
+    sweep(m4, m3, rhs1, cond, gain1, middle, 2)
+    receive(m3, 7, m4, 1, cond, gain1, middle)
+    send(m4, 8)
+
+    def last_middle(z, _):
+        centre, left = residual(m4, z, rhs1[z], cond[z], middle, 2)
+        inner = slice(1, block + 1)
+        a3[z + 1, inner] = a2[z + 1, inner] + (centre + gain1[z] * left)
+        return 0
+
+    lax.fori_loop(0, planes, last_middle, 0)
+    receive(m4, 8, a3, 1, cond, gain1, middle)
+    send(a3, 9)
+    sweep(a4, a3, rhs, cond, gain0, fine, 1)
+    receive(a3, 9, a4, 1, cond, gain0, fine)
+    send(a4, 10)
+    sweep(a5, a4, rhs, cond, gain0, fine, 1)
+    receive(a4, 10, a5, 1, cond, gain0, fine)
+    send(a5, 11)
+
+    def outward(which, src, off, dst, peer, owner):
+        inner, deep = pl.ds(off, block), pl.ds(off, planes)
+        return pltpu.make_async_remote_copy(
+            src_ref=src.at[deep, inner, peer, :],
+            dst_ref=dst.at[:, rows_of(owner), :],
+            send_sem=out_send.at[which, peer],
+            recv_sem=out_recv.at[which, owner],
+            device_id={"tm": peer},
+            device_id_type=MESH,
+        )
+
+    def home(which, src, off, dst):
+        return pltpu.make_async_copy(
+            src.at[pl.ds(off, planes), pl.ds(off, block), me, :],
+            dst.at[:, rows_of(me), :],
+            out_own.at[which],
+        )
+
+    for k in order:
+        outward(0, a5, 1, out_solution, me ^ k, me).start()
+    home(0, a5, 1, out_solution).start()
+    defect_into(fd, 0, a5, rhs, cond, fine, 1)
+    receive(a5, 11, fd, 0, cond, None, fine)
+    for k in order:
+        outward(1, fd, 0, out_defect, me ^ k, me).start()
+    home(1, fd, 0, out_defect).start()
+
+    for ref, stage in sent:
+        for sends, _, copy in faces(ref, stage):
+            pl.when(sends)(copy.wait_send)
+    for k in order:
+        inward(me ^ k, me, me).wait_send()
+    for which, src, off, dst in ((0, a5, 1, out_solution), (1, fd, 0, out_defect)):
+        home(which, src, off, dst).wait()
+        for k in order:
+            outward(which, src, off, dst, me ^ k, me).wait_send()
+            outward(which, src, off, dst, me, me ^ k).wait_recv()
+
+
+def fused_body(peers, slabs, source, conductivity):
+    _, planes, rows, lanes = source.shape
+    block = rows // peers
+
+    def field(depth, width):
+        return pltpu.VMEM((depth, width, peers, lanes), jnp.float32)
+
+    plain, framed = field(planes, block), field(planes + 2, block + 2)
+    small, small_framed = (
+        field(planes // 2, block // 2),
+        field(planes // 2 + 2, block // 2 + 2),
+    )
+    dma = pltpu.SemaphoreType.DMA
+    vmem, anywhere = pl.BlockSpec(memory_space=pltpu.VMEM), pl.BlockSpec(memory_space=pl.ANY)
+    shape = jax.ShapeDtypeStruct((planes, rows, lanes), jnp.float32)
+
+    def faces_of(slots, depth):
+        return pltpu.VMEM((slots, 2, depth, peers, lanes), jnp.float32)
+
+    solution, final_defect = pl.pallas_call(
+        functools.partial(cycle_kernel, peers, slabs),
+        out_shape=(shape, shape),
+        in_specs=[vmem, anywhere, vmem],
+        out_specs=(anywhere, anywhere),
+        scratch_shapes=[
+            plain, plain, small, plain,
+            plain, small, plain, plain, small,
+            framed, framed, framed, framed, framed, plain,
+            framed, framed, framed, framed,
+            small_framed, small_framed, small_framed, small_framed,
+            faces_of(9, block), faces_of(9, planes),
+            faces_of(3, block // 2), faces_of(3, planes // 2),
+            dma((peers,)), dma((peers,)), dma,
+            dma((12, 4)), dma((12, 4)),
+            dma((2, peers)), dma((2, peers)), dma((2,)),
+        ],
+        compiler_params=pltpu.CompilerParams(
+            collective_id=0, has_side_effects=True, vmem_limit_bytes=32 * 1024 * 1024
+        ),
+    )(source[0], source[0], conductivity)
+    return (solution[None], final_defect[None])
+
+
 def solution(mesh):
+    peers, slabs = mesh.shape["tm"], mesh.shape["space"]
+
+    def chosen(source, conductivity):
+        steps, planes, rows, lanes = source.shape
+        if fits(steps * peers, peers, slabs, planes, rows, lanes):
+            return fused_body(peers, slabs, source, conductivity)
+        return body(source, conductivity)
+
     return jax.shard_map(
-        body,
+        chosen,
         mesh=mesh,
         in_specs=(P("tm", "space", None, None), P("space", None, None)),
         out_specs=(P("tm", "space", None, None), P("tm", "space", None, None)),

time: 239 us -> 82.7 us (0.35); the launches traced: 235 us -> 82.5 us
  starting transfers between devices: 133 us -> 0 us
  Pallas kernels: 0 us -> 78.2 us
  waiting for transfers between devices: 67.7 us -> 0 us
  other arithmetic: 17.1 us -> 0 us
  local copies, waits for them, and re-layouts: 15.8 us -> 3.66 us
    ppermute x45 -> x0, starting transfers between devices: 133 us -> none  [the longest x15 65.6 us: shifted(): return lax.ppermute(shard, axis, pairs)]
    pallas_call x0 -> x1, Pallas kernels: none -> 78.2 us  [fused_body(): pl.pallas_call(functools.partial(cycle_kernel, peers, slabs), out_shape=(...]
    ppermute x45 -> x0, waiting for transfers between devices: 67.7 us -> none  [the longest x15 54.9 us: shifted(): return lax.ppermute(shard, axis, pairs)]
    slice x35 -> x0, local copies, waits for them, and re-layouts: 14.3 us -> none  [the longest x2 3.16 us: coarsen(): values[..., 1::2, 1::2, :]]
    add x11 -> x0, other arithmetic: 6.41 us -> none  [the longest x8 3.81 us: relaxed(): current + OMEGA * defect(current, right_side, earlier, padded, conduct, s...]
    concatenate x14 -> x0, other arithmetic: 5.63 us -> none  [padded_2(): shard = jnp.concatenate([before, shard, after], axis=dim)]
    unnamed x8 -> x6, local copies, waits for them, and re-layouts: 0.63 us -> 3.66 us
  transfers between devices with their start and end apart: 45 -> 0, of which waited for: 24 -> 0; matrix products, arithmetic and copies ran while one was open for 10% -> 0% of each run, Pallas kernels for 0% -> 0%
where the time goes in v1:
time: 82.7 us; the launch traced here: 82.5 us
  Pallas kernels  78.2 us (95%)
  local copies, waits for them, and re-layouts  3.66 us (4%)
    pallas_call x1, Pallas kernels, fused_body(): pl.pallas_call(functools.partial(cycle_kernel, peers, slabs), out_shape=(...  78.2 us
    unnamed x6, local copies, waits for them, and re-layouts  3.66 us

profile of v1, /device:TPU:0, one launch (start us, length us, event | category | flops | bytes accessed | tf_op | source)
XLA Modules:
  0.0 82.5 jit_solution(2226014429133109975)
XLA Ops:
  0.6 0.0 copy-start
  0.6 1.0 %copy-done = f32[1,8,128,128]{3,2,1,0:T(8,128)S(1)} copy-done((f32[1,8,128,128]{3,2,1,0:T(8,128)S(1)}, f32[1,8,128,128]{3,2,1,0:T(8,128)}, u32[]{:S(2)}) %copy-start) | copy-done | bytes 524312
  1.7 0.0 copy-start.1
  1.7 1.0 %copy-done.1 = f32[8,128,128]{2,1,0:T(8,128)S(1)} copy-done((f32[8,128,128]{2,1,0:T(8,128)S(1)}, f32[8,128,128]{2,1,0:T(8,128)}, u32[]{:S(2)}) %copy-start.1) | copy-done | bytes 524312
  2.7 78.2 %shard_map.41 = (f32[8,128,128]{2,1,0:T(8,128)S(1)}, f32[8,128,128]{2,1,0:T(8,128)S(1)}) custom-call(f32[8,128,128]{2,1,0:T(8,128)S(1)} %bitcast.3, f32[8,128,128]{2,1,0:T(8,128)S(1)} %bitcast.4, f32[8,128,128]{2,1,0:T(8,128)S(1)} %copy-done.1), custom_call_target="tpu_custom_call" | custom-call | tf_op jit(solution)/shard_map/pallas_call | solution.py:550
  80.9 0.8 copy.6
  81.7 0.8 copy.7
Async XLA Ops:
  0.6 1.0 %copy-start = (f32[1,8,128,128]{3,2,1,0:T(8,128)S(1)}, f32[1,8,128,128]{3,2,1,0:T(8,128)}, u32[]{:S(2)}) copy-start(f32[1,8,128,128]{3,2,1,0:T(8,128)} %param.2) | copy-start | bytes 1572868
  1.7 1.0 %copy-start.1 = (f32[8,128,128]{2,1,0:T(8,128)S(1)}, f32[8,128,128]{2,1,0:T(8,128)}, u32[]{:S(2)}) copy-start(f32[8,128,128]{2,1,0:T(8,128)} %conduct.1) | copy-start | bytes 1572868

commit v2 on v1

--- a/solution.py
+++ b/solution.py
@@ -191,9 +191,8 @@
 def cycle_kernel(
     peers,
     slabs,
-    source,
     source_far,
-    conduct,
+    conduct_far,
     out_solution,
     out_defect,
     rhs, rhs1, rhs2, scrap,
@@ -202,7 +201,8 @@
     m1, m2, m3, m4,
     k1, k2, k3, k4,
     halo_z, halo_x, halo_z2, halo_x2,
-    in_send, in_recv, own_sem,
+    source, conduct,
+    in_send, in_recv, own_sem, load_sem,
     h_send, h_recv,
     out_send, out_recv, out_own,
 ):
@@ -215,6 +215,10 @@
     has_next, has_prev = mine < peers - 1, mine > 0
     has_up, has_down = slab < slabs - 1, slab > 0
 
+    load_source = pltpu.make_async_copy(source_far, source, load_sem.at[0])
+    load_conduct = pltpu.make_async_copy(conduct_far, conduct, load_sem.at[1])
+    load_source.start()
+    load_conduct.start()
     barrier = pltpu.get_barrier_semaphore()
     for k in range(1, peers):
         pl.semaphore_signal(
@@ -230,6 +234,7 @@
         pl.semaphore_signal(barrier, inc=1, device_id={"space": slab - 1}, device_id_type=MESH)
 
     neighbours = jnp.where(has_up, 1, 0) + jnp.where(has_down, 1, 0)
+    load_source.wait()
     pl.semaphore_wait(barrier, peers - 1 + neighbours)
 
     def rows_of(index):
@@ -252,6 +257,8 @@
         source_far.at[:, rows_of(me), :], rhs.at[:, :, me, :], own_sem
     )
     own.start()
+
+    load_conduct.wait()
 
     def fill(z, _):
         for x in range(block):
@@ -407,30 +414,46 @@
 
     fine, middle, coarse = FINE, scaled(FINE, 2.0), scaled(COARSE, 4.0)
 
+    def edges_first(depth, width, work, between):
+        work(0, 0, width)
+        work(depth - 1, 0, width)
+
+        def sides(z, _):
+            work(z, 0, 1)
+            work(z, width - 1, 1)
+            return 0
+
+        lax.fori_loop(1, depth - 1, sides, 0)
+        between()
+
+        def rest(z, _):
+            work(z, 1, width - 2)
+            return 0
+
+        lax.fori_loop(1, depth - 1, rest, 0)
+
     own.wait()
     for k in order:
         inward(me, me ^ k, me ^ k).wait_recv()
 
-    def first(z, _):
-        a1[z + 1, 1 : block + 1] = gain0[z] * rhs[z]
-        return 0
-
-    lax.fori_loop(0, planes, first, 0)
-    send(a1, 0)
+    def first(z, x, count):
+        at = slice(x, x + count)
+        a1[z + 1, x + 1 : x + 1 + count] = gain0[z, at] * rhs[z, at]
+
+    edges_first(planes, block, first, lambda: send(a1, 0))
     sweep(a2, a1, rhs, cond, gain0, fine, 1)
     receive(a1, 0, a2, 1, cond, gain0, fine)
     send(a2, 1)
     defect_into(scrap, 0, a2, rhs, cond, fine, 1)
     receive(a2, 1, scrap, 0, cond, None, fine)
 
-    def restrict_time(z, _):
-        value = with_partner(scrap[z], 1)
-        rhs1[z] = value
-        m1[z + 1, 1 : block + 1] = gain1[z] * value
-        return 0
-
-    lax.fori_loop(0, planes, restrict_time, 0)
-    send(m1, 2)
+    def restrict_time(z, x, count):
+        at = slice(x, x + count)
+        value = with_partner(scrap[z, at], 1)
+        rhs1[z, at] = value
+        m1[z + 1, x + 1 : x + 1 + count] = gain1[z, at] * value
+
+    edges_first(planes, block, restrict_time, lambda: send(m1, 2))
     sweep(m2, m1, rhs1, cond, gain1, middle, 2)
     receive(m1, 2, m2, 1, cond, gain1, middle)
     send(m2, 3)
@@ -458,17 +481,15 @@
     sweep(k4, k3, rhs2, cond2, gain2, coarse, 4)
     receive(k3, 6, k4, 1, cond2, gain2, coarse)
 
-    def prolong(z, _):
-        for x in range(half_block):
-            value = k4[z + 1, x + 1]
+    def prolong(z, x, count):
+        for near in range(x, x + count):
+            value = k4[z + 1, near + 1]
             for dz in range(2):
                 for dx in range(2):
-                    at = (2 * z + dz + 1, 2 * x + dx + 1)
+                    at = (2 * z + dz + 1, 2 * near + dx + 1)
                     m3[at] = m2[at] + value
-        return 0
-
-    lax.fori_loop(0, half_planes, prolong, 0)
-    send(m3, 7)
+
+    edges_first(half_planes, half_block, prolong, lambda: send(m3, 7))
     sweep(m4, m3, rhs1, cond, gain1, middle, 2)
     receive(m3, 7, m4, 1, cond, gain1, middle)
     send(m4, 8)
@@ -484,48 +505,65 @@
     send(a3, 9)
     sweep(a4, a3, rhs, cond, gain0, fine, 1)
     receive(a3, 9, a4, 1, cond, gain0, fine)
+    whole = (0, planes, 0, block)
+    centre_part = (1, planes - 2, 1, block - 2)
+    edge_parts = (
+        (0, 1, 0, block),
+        (planes - 1, 1, 0, block),
+        (1, planes - 2, 0, 1),
+        (1, planes - 2, block - 1, 1),
+    )
+    pieces = [(a5, 1, out_solution, part) for part in (centre_part,) + edge_parts]
+    pieces.append((fd, 0, out_defect, whole))
+
+    def ends(piece, step, owner):
+        src, off, dst, (z, deep, x, wide) = pieces[piece]
+        return (
+            src.at[pl.ds(z + off, deep), pl.ds(x + off, wide), step, :],
+            dst.at[pl.ds(z, deep), pl.ds(snake(owner) * block + x, wide), :],
+        )
+
+    def outward(piece, peer, owner):
+        src, dst = ends(piece, peer, owner)
+        return pltpu.make_async_remote_copy(
+            src_ref=src,
+            dst_ref=dst,
+            send_sem=out_send.at[piece, peer],
+            recv_sem=out_recv.at[piece, owner],
+            device_id={"tm": peer},
+            device_id_type=MESH,
+        )
+
+    def home(piece):
+        src, dst = ends(piece, me, me)
+        return pltpu.make_async_copy(src, dst, out_own.at[piece])
+
+    def ship(piece):
+        for k in order:
+            outward(piece, me ^ k, me).start()
+        home(piece).start()
+
     send(a4, 10)
     sweep(a5, a4, rhs, cond, gain0, fine, 1)
+    ship(0)
     receive(a4, 10, a5, 1, cond, gain0, fine)
     send(a5, 11)
-
-    def outward(which, src, off, dst, peer, owner):
-        inner, deep = pl.ds(off, block), pl.ds(off, planes)
-        return pltpu.make_async_remote_copy(
-            src_ref=src.at[deep, inner, peer, :],
-            dst_ref=dst.at[:, rows_of(owner), :],
-            send_sem=out_send.at[which, peer],
-            recv_sem=out_recv.at[which, owner],
-            device_id={"tm": peer},
-            device_id_type=MESH,
-        )
-
-    def home(which, src, off, dst):
-        return pltpu.make_async_copy(
-            src.at[pl.ds(off, planes), pl.ds(off, block), me, :],
-            dst.at[:, rows_of(me), :],
-            out_own.at[which],
-        )
-
-    for k in order:
-        outward(0, a5, 1, out_solution, me ^ k, me).start()
-    home(0, a5, 1, out_solution).start()
+    for piece in range(1, 5):
+        ship(piece)
     defect_into(fd, 0, a5, rhs, cond, fine, 1)
     receive(a5, 11, fd, 0, cond, None, fine)
-    for k in order:
-        outward(1, fd, 0, out_defect, me ^ k, me).start()
-    home(1, fd, 0, out_defect).start()
+    ship(5)
 
     for ref, stage in sent:
         for sends, _, copy in faces(ref, stage):
             pl.when(sends)(copy.wait_send)
     for k in order:
         inward(me ^ k, me, me).wait_send()
-    for which, src, off, dst in ((0, a5, 1, out_solution), (1, fd, 0, out_defect)):
-        home(which, src, off, dst).wait()
+    for piece in range(6):
+        home(piece).wait()
         for k in order:
-            outward(which, src, off, dst, me ^ k, me).wait_send()
-            outward(which, src, off, dst, me, me ^ k).wait_recv()
+            outward(piece, me ^ k, me).wait_send()
+            outward(piece, me, me ^ k).wait_recv()
 
 
 def fused_body(peers, slabs, source, conductivity):
@@ -541,7 +579,8 @@
         field(planes // 2 + 2, block // 2 + 2),
     )
     dma = pltpu.SemaphoreType.DMA
-    vmem, anywhere = pl.BlockSpec(memory_space=pltpu.VMEM), pl.BlockSpec(memory_space=pl.ANY)
+    anywhere = pl.BlockSpec(memory_space=pl.ANY)
+    slab = pltpu.VMEM((planes, rows, lanes), jnp.float32)
     shape = jax.ShapeDtypeStruct((planes, rows, lanes), jnp.float32)
 
     def faces_of(slots, depth):
@@ -550,7 +589,7 @@
     solution, final_defect = pl.pallas_call(
         functools.partial(cycle_kernel, peers, slabs),
         out_shape=(shape, shape),
-        in_specs=[vmem, anywhere, vmem],
+        in_specs=[anywhere, anywhere],
         out_specs=(anywhere, anywhere),
         scratch_shapes=[
             plain, plain, small, plain,
@@ -560,14 +599,15 @@
             small_framed, small_framed, small_framed, small_framed,
             faces_of(9, block), faces_of(9, planes),
             faces_of(3, block // 2), faces_of(3, planes // 2),
-            dma((peers,)), dma((peers,)), dma,
+            slab, slab,
+            dma((peers,)), dma((peers,)), dma, dma((2,)),
             dma((12, 4)), dma((12, 4)),
-            dma((2, peers)), dma((2, peers)), dma((2,)),
+            dma((6, peers)), dma((6, peers)), dma((6,)),
         ],
         compiler_params=pltpu.CompilerParams(
-            collective_id=0, has_side_effects=True, vmem_limit_bytes=32 * 1024 * 1024
+            collective_id=0, has_side_effects=True, vmem_limit_bytes=60 * 1024 * 1024
         ),
-    )(source[0], source[0], conductivity)
+    )(source[0], conductivity)
     return (solution[None], final_defect[None])
 
 

time: 82.7 us -> 80.7 us (0.976)
  Pallas kernels: 78.2 us -> 77.1 us
  local copies, waits for them, and re-layouts: 3.66 us -> 2.73 us
    pallas_call x1, Pallas kernels: 78.2 us -> 77.1 us  [fused_body(): pl.pallas_call(functools.partial(cycle_kernel, peers, slabs), out_shape=(...]
    unnamed x6 -> x4, local copies, waits for them, and re-layouts: 3.66 us -> 2.73 us
where the time goes in v2:
time: 80.7 us; the launch traced here: 80.5 us
  Pallas kernels  77.1 us (96%)
  local copies, waits for them, and re-layouts  2.73 us (3%)
    pallas_call x1, Pallas kernels, fused_body(): pl.pallas_call(functools.partial(cycle_kernel, peers, slabs), out_shape=(...  77.1 us
    unnamed x4, local copies, waits for them, and re-layouts  2.73 us

profile of v2, /device:TPU:0, one launch (start us, length us, event | category | flops | bytes accessed | tf_op | source)
XLA Modules:
  0.0 80.5 jit_solution(15102508419566187377)
XLA Ops:
  0.6 77.1 %shard_map.41 = (f32[8,128,128]{2,1,0:T(8,128)}, f32[8,128,128]{2,1,0:T(8,128)}) custom-call(f32[8,128,128]{2,1,0:T(8,128)} %bitcast.3, f32[8,128,128]{2,1,0:T(8,128)} %conduct_far.1), custom_call_target="tpu_custom_call" | custom-call | tf_op jit(solution)/shard_map/pallas_call | solution.py:589
  77.8 0.0 copy-start
  77.8 1.9 %copy.6 = f32[1,8,128,128]{3,2,1,0:T(8,128)} copy(f32[1,8,128,128]{3,2,1,0:T(8,128)} %bitcast.5) | data formatting | bytes 1048576
  79.7 0.0 copy-done
  79.7 0.8 copy.7
Async XLA Ops:
  77.8 1.9 %copy-start = (f32[8,128,128]{2,1,0:T(8,128)S(1)}, f32[8,128,128]{2,1,0:T(8,128)}, u32[]{:S(2)}) copy-start(f32[8,128,128]{2,1,0:T(8,128)} %get-tuple-element.5) | copy-start | bytes 1572868

commit v3 on v0

--- a/solution.py
+++ b/solution.py
@@ -1,6 +1,10 @@
+import functools
+
 import jax
 import jax.numpy as jnp
 from jax import lax
+from jax.experimental import pallas as pl
+from jax.experimental.pallas import tpu as pltpu
 from jax.sharding import PartitionSpec as P
 
 NU = 2
@@ -158,9 +162,485 @@
     return (solution[None], final_defect[None])
 
 
+MESH = pl.DeviceIdType.MESH
+
+
+def snake(index):
+    return index + ((index // 2) % 2) * (1 - 2 * (index % 2))
+
+
+def scaled(weights, stretch):
+    return tuple(stretch * weight for weight in weights)
+
+
+def fits(steps, peers, slabs, planes, rows, lanes):
+    block = rows // peers
+    return (
+        steps == peers
+        and peers % 8 == 0
+        and peers & (peers - 1) == 0
+        and rows % peers == 0
+        and block % 8 == 0
+        and planes % 2 == 0
+        and planes >= 6
+        and lanes % 128 == 0
+        and peers <= 16
+        and slabs > 1
+    )
+
+
+PAD, PAD2 = 2, 3
+
+
+def cycle_kernel(
+    peers,
+    slabs,
+    source_far,
+    conduct_far,
+    out_solution,
+    out_defect,
+    rhs, rhs1, rhs2, scrap,
+    cond, cond2, gain0, gain1, gain2,
+    a1, a2, a3, a4, a5, fd,
+    m1, m2, m3, m4,
+    k1, k2, k3, k4,
+    source, tall,
+    in_send, in_recv, own_sem, load_sem,
+    tall_send, tall_recv,
+    h_send, h_recv,
+    out_send, out_recv, out_own,
+):
+    planes, rows, lanes = source.shape
+    block = rows // peers
+    half_planes, half_block = planes // 2, block // 2
+    reach = 2 * PAD2
+    me, slab = lax.axis_index("tm"), lax.axis_index("space")
+    mine = snake(me)
+    following, preceding = snake((mine + 1) % peers), snake((mine + peers - 1) % peers)
+    has_z = {1: slab < slabs - 1, -1: slab > 0, 0: None}
+    has_x = {1: mine < peers - 1, -1: mine > 0, 0: None}
+    beside = {1: following, -1: preceding}
+
+    def both(first, second):
+        if first is None:
+            return second
+        return first if second is None else first & second
+
+    def device(dz, dx):
+        where = {}
+        if dx:
+            where["tm"] = beside[dx]
+        if dz:
+            where["space"] = slab + dz
+        return where
+
+    def size_of(ref):
+        pad = PAD2 if ref.shape[0] == half_planes + 2 * PAD2 else PAD
+        return pad, ref.shape[0] - 2 * pad, ref.shape[1] - 2 * pad
+
+    def box(ref, ring):
+        pad, depth, width = size_of(ref)
+        return (pad - ring, pad + depth + ring, pad - ring, pad + width + ring)
+
+    def strips(ref, outer, inner):
+        z0, z1, x0, x1 = box(ref, outer)
+        i0, i1, j0, j1 = box(ref, inner)
+        return ((z0, i0, x0, x1), (i1, z1, x0, x1), (i0, i1, x0, j0), (i0, i1, j1, x1))
+
+    def over(boxes, work):
+        for z0, z1, x0, x1 in boxes:
+
+            def step(z, _, x0=x0, x1=x1):
+                work(z, x0, x1)
+                return 0
+
+            lax.fori_loop(z0, z1, step, 0)
+
+    load_source = pltpu.make_async_copy(source_far, source, load_sem.at[0])
+    load_conduct = pltpu.make_async_copy(
+        conduct_far, tall.at[pl.ds(reach, planes)], load_sem.at[1]
+    )
+    load_source.start()
+    load_conduct.start()
+
+    for ref in (rhs, rhs1, m3, a3, a5, rhs2):
+
+        def clear(z, x0, x1, ref=ref):
+            ref[z, x0:x1] = jnp.zeros((x1 - x0, peers, lanes), jnp.float32)
+
+        over(strips(ref, size_of(ref)[0], 0), clear)
+
+    barrier = pltpu.get_barrier_semaphore()
+    for k in range(1, peers):
+        pl.semaphore_signal(barrier, inc=1, device_id={"tm": me ^ k}, device_id_type=MESH)
+    expected = peers - 1
+    for dz in (1, -1):
+        for dx in (0, 1, -1):
+            here = both(has_z[dz], has_x[dx])
+
+            @pl.when(here)
+            def _(dz=dz, dx=dx):
+                pl.semaphore_signal(
+                    barrier, inc=1, device_id=device(dz, dx), device_id_type=MESH
+                )
+
+            expected = expected + jnp.where(here, 1, 0)
+    load_source.wait()
+    pl.semaphore_wait(barrier, expected)
+
+    def rows_of(index):
+        return pl.ds(pl.multiple_of(snake(index) * block, 8), block)
+
+    def inward(peer, step, recv):
+        return pltpu.make_async_remote_copy(
+            src_ref=source.at[:, rows_of(peer), :],
+            dst_ref=rhs.at[pl.ds(PAD, planes), pl.ds(PAD, block), step, :],
+            send_sem=in_send.at[peer],
+            recv_sem=in_recv.at[recv],
+            device_id={"tm": peer},
+            device_id_type=MESH,
+        )
+
+    order = sorted(range(1, peers), reverse=True)
+    for k in order:
+        inward(me ^ k, me, me).start()
+    own = pltpu.make_async_copy(
+        source_far.at[:, rows_of(me), :],
+        rhs.at[pl.ds(PAD, planes), pl.ds(PAD, block), me, :],
+        own_sem,
+    )
+    own.start()
+    load_conduct.wait()
+
+    def tall_copy(side, dz):
+        src = planes if dz > 0 else reach
+        dst = 0 if dz > 0 else reach + planes
+        return pltpu.make_async_remote_copy(
+            src_ref=tall.at[pl.ds(src, reach)],
+            dst_ref=tall.at[pl.ds(dst, reach)],
+            send_sem=tall_send.at[side],
+            recv_sem=tall_recv.at[side],
+            device_id={"space": slab + dz},
+            device_id_type=MESH,
+        )
+
+    for side, dz in ((0, 1), (1, -1)):
+        pl.when(has_z[dz])(tall_copy(side, dz).start)
+    for side, dz in ((0, 1), (1, -1)):
+        pl.when(has_z[-dz])(tall_copy(side, dz).wait_recv)
+
+        @pl.when(jnp.logical_not(has_z[-dz]))
+        def _(dz=dz):
+            start = 0 if dz > 0 else reach + planes
+            tall[start : start + reach] = jnp.zeros((reach, rows, lanes), jnp.float32)
+
+    def inside(z, x, factor):
+        plane = slab * (planes // factor) + z
+        row = mine * (block // factor) + x
+        ok = (plane >= 0) & (plane < slabs * planes // factor)
+        ok = ok & (row >= 0) & (row < rows // factor)
+        return jnp.where(ok, 1.0, 0.0)
+
+    def fill(z, _):
+        for x in range(block + 2 * PAD):
+            row = jnp.clip(mine * block + x - PAD, 0, rows - 1)
+            value = jnp.broadcast_to(tall[z + reach - PAD, pl.ds(row, 1), :], (peers, lanes))
+            mask = inside(z - PAD, x - PAD, 1)
+            cond[z, x] = value * mask
+            gain0[z, x] = mask * (OMEGA / (1.0 + value * (2.0 * sum(FINE))))
+            gain1[z, x] = mask * (OMEGA / (1.0 + value * (4.0 * sum(FINE))))
+        return 0
+
+    lax.fori_loop(0, planes + 2 * PAD, fill, 0)
+
+    def fill2(z, _):
+        for x in range(half_block + 2 * PAD2):
+            row = jnp.clip(mine * block + 2 * (x - PAD2), 0, rows - 2)
+            quad = (tall[2 * z, pl.ds(row, 1), :] + tall[2 * z + 1, pl.ds(row, 1), :]) + (
+                tall[2 * z, pl.ds(row + 1, 1), :] + tall[2 * z + 1, pl.ds(row + 1, 1), :]
+            )
+            value = jnp.broadcast_to(0.25 * quad, (peers, lanes))
+            mask = inside(z - PAD2, x - PAD2, 2)
+            cond2[z, x] = value * mask
+            gain2[z, x] = mask * (OMEGA / (1.0 + value * (8.0 * sum(COARSE))))
+        return 0
+
+    lax.fori_loop(0, half_planes + 2 * PAD2, fill2, 0)
+
+    time = lax.broadcasted_iota(jnp.int32, (1, peers, lanes), 1)
+    lane = lax.broadcasted_iota(jnp.int32, (1, peers, lanes), 2)
+    not_first, not_last = lane > 0, lane < lanes - 1
+
+    def prior(value, shift):
+        return jnp.where(time >= shift, pltpu.roll(value, shift, 1), 0.0)
+
+    def with_partner(value, shift):
+        even = (time // shift) % 2 == 0
+        return value + jnp.where(
+            even, pltpu.roll(value, peers - shift, 1), pltpu.roll(value, shift, 1)
+        )
+
+    def residual(ref, z, x0, x1, right, conductivity, weights, shift):
+        weight_z, weight_x, weight_y = weights
+        at = slice(x0, x1)
+        centre = ref[z, at]
+        along_z = ref[z - 1, at] + ref[z + 1, at]
+        along_x = ref[z, x0 - 1 : x1 - 1] + ref[z, x0 + 1 : x1 + 1]
+        along_y = jnp.where(not_first, pltpu.roll(centre, 1, 2), 0.0) + jnp.where(
+            not_last, pltpu.roll(centre, lanes - 1, 2), 0.0
+        )
+        if weight_z == weight_x == weight_y:
+            around = weight_z * (6.0 * centre - (along_z + along_x + along_y))
+        else:
+            around = (2.0 * (weight_z + weight_x + weight_y)) * centre - (
+                weight_z * along_z + weight_x * along_x + weight_y * along_y
+            )
+        left = right[z, at] + prior(centre, shift) - centre - conductivity[z, at] * around
+        return centre, left
+
+    def sweeper(new, old, right, conductivity, gain, weights, shift, base=None):
+        def work(z, x0, x1):
+            centre, left = residual(old, z, x0, x1, right, conductivity, weights, shift)
+            value = centre + gain[z, x0:x1] * left
+            new[z, x0:x1] = value if base is None else base[z, x0:x1] + value
+
+        return work
+
+    def starter(new, right, gain):
+        def work(z, x0, x1):
+            new[z, x0:x1] = gain[z, x0:x1] * right[z, x0:x1]
+
+        return work
+
+    def defecter(new, old, right, weights, shift, pairs):
+        def work(z, x0, x1):
+            left = residual(old, z, x0, x1, right, cond, weights, shift)[1]
+            new[z, x0:x1] = with_partner(left, 1) if pairs else left
+
+        return work
+
+    def wide(ref, depth, corner, stage):
+        pad, deep, broad = size_of(ref)
+
+        def spans(step, size, count):
+            if step == 0:
+                return pl.ds(pad, size), pl.ds(pad, size)
+            if step > 0:
+                return pl.ds(pad + size - count, count), pl.ds(pad - count, count)
+            return pl.ds(pad, count), pl.ds(pad + size, count)
+
+        out = []
+        steps = [(dz, dx) for dz in (1, -1) for dx in (1, -1)] if corner else []
+        for number, (dz, dx) in enumerate(steps + [(0, 1), (0, -1), (1, 0), (-1, 0)]):
+            count = corner if dz and dx else depth
+            src_z, dst_z = spans(dz, deep, count)
+            src_x, dst_x = spans(dx, broad, count)
+            copy = pltpu.make_async_remote_copy(
+                src_ref=ref.at[src_z, src_x],
+                dst_ref=ref.at[dst_z, dst_x],
+                send_sem=h_send.at[stage, number],
+                recv_sem=h_recv.at[stage, number],
+                device_id=device(dz, dx),
+                device_id_type=MESH,
+            )
+            sends = both(has_z[dz], has_x[dx])
+            arrives = both(has_z[-dz], has_x[-dx])
+            out.append((sends, arrives, copy))
+        return out
+
+    started = []
+
+    def send(ref, depth, corner, stage):
+        copies = wide(ref, depth, corner, stage)
+        for sends, _, copy in copies:
+            pl.when(sends)(copy.start)
+        started.append(copies)
+
+    def receive():
+        for _, arrives, copy in started[-1]:
+            pl.when(arrives)(copy.wait_recv)
+
+    fine, middle, coarse = FINE, scaled(FINE, 2.0), scaled(COARSE, 4.0)
+
+    def pieces_of(ref, edge):
+        _, deep, broad = size_of(ref)
+        return (
+            (edge, deep - 2 * edge, edge, broad - 2 * edge),
+            (0, edge, 0, broad),
+            (deep - edge, edge, 0, broad),
+            (edge, deep - 2 * edge, 0, edge),
+            (edge, deep - 2 * edge, broad - edge, edge),
+        )
+
+    pieces = [(a5, out_solution, part) for part in pieces_of(a5, 2)]
+    pieces.append((fd, out_defect, (0, planes, 0, block)))
+
+    def ends(piece, step, owner):
+        src, dst, (z, deep, x, broad) = pieces[piece]
+        return (
+            src.at[pl.ds(z + PAD, deep), pl.ds(x + PAD, broad), step, :],
+            dst.at[pl.ds(z, deep), pl.ds(snake(owner) * block + x, broad), :],
+        )
+
+    def outward(piece, peer, owner):
+        src, dst = ends(piece, peer, owner)
+        return pltpu.make_async_remote_copy(
+            src_ref=src,
+            dst_ref=dst,
+            send_sem=out_send.at[piece, peer],
+            recv_sem=out_recv.at[piece, owner],
+            device_id={"tm": peer},
+            device_id_type=MESH,
+        )
+
+    def home(piece):
+        src, dst = ends(piece, me, me)
+        return pltpu.make_async_copy(src, dst, out_own.at[piece])
+
+    def ship(piece):
+        for k in order:
+            outward(piece, me ^ k, me).start()
+        home(piece).start()
+
+    def stages(boxes_of, works):
+        for work, (ref, rings) in zip(works, boxes_of):
+            over(strips(ref, *rings) if isinstance(rings, tuple) else (box(ref, rings),), work)
+
+    def presmooth(x, right, one, two, left, gain, weights, shift, pairs):
+        works = (
+            starter(one, right, gain),
+            sweeper(two, one, right, cond, gain, weights, shift),
+            defecter(left, two, right, weights, shift, pairs),
+        )
+        send(right, 2, 1, x)
+        stages(((one, 0), (two, -1), (left, -2)), works)
+        receive()
+        stages(((one, (2, 0)), (two, (1, -1)), (left, (0, -2))), works)
+
+    own.wait()
+    for k in order:
+        inward(me, me ^ k, me ^ k).wait_recv()
+    presmooth(0, rhs, a1, a2, rhs1, gain0, fine, 1, True)
+    presmooth(1, rhs1, m1, m2, scrap, gain1, middle, 2, False)
+
+    def restrict(z, _):
+        for x in range(half_block):
+            zz, xx = 2 * z + PAD, 2 * x + PAD
+            quad = (scrap[zz, xx] + scrap[zz + 1, xx]) + (
+                scrap[zz, xx + 1] + scrap[zz + 1, xx + 1]
+            )
+            rhs2[z + PAD2, x + PAD2] = 0.25 * with_partner(quad[None], 2)[0]
+        return 0
+
+    lax.fori_loop(0, half_planes, restrict, 0)
+    send(rhs2, 3, 2, 2)
+    start = starter(k1, rhs2, gain2)
+    works = [
+        sweeper(new, old, rhs2, cond2, gain2, coarse, 4)
+        for new, old in ((k2, k1), (k3, k2), (k4, k3))
+    ]
+    stages(((k1, 0), (k2, -1)), (start, works[0]))
+    receive()
+    stages(((k1, (3, 0)), (k2, (2, -1)), (k3, 1), (k4, 0)), (start, *works))
+
+    def prolong(z, x0, x1):
+        for x in range(x0, x1):
+            value = k4[z, x]
+            for dz in range(2):
+                for dx in range(2):
+                    at = (2 * (z - PAD2) + dz + PAD, 2 * (x - PAD2) + dx + PAD)
+                    m3[at] = m2[at] + value
+
+    over(strips(k4, 0, -1), prolong)
+    send(m3, 2, 1, 3)
+    over((box(k4, -1),), prolong)
+    works = (
+        sweeper(m4, m3, rhs1, cond, gain1, middle, 2),
+        sweeper(a3, m4, rhs1, cond, gain1, middle, 2, a2),
+    )
+    stages(((m4, -1), (a3, -2)), works)
+    receive()
+    stages(((m4, (1, -1)), (a3, (0, -2))), works)
+    send(a3, 2, 1, 4)
+    works = (
+        sweeper(a4, a3, rhs, cond, gain0, fine, 1),
+        sweeper(a5, a4, rhs, cond, gain0, fine, 1),
+    )
+    stages(((a4, -1), (a5, -2)), works)
+    ship(0)
+    receive()
+    stages(((a4, (1, -1)), (a5, (0, -2))), works)
+    send(a5, 1, 0, 5)
+    for piece in range(1, 5):
+        ship(piece)
+    works = (defecter(fd, a5, rhs, fine, 1, False),)
+    stages(((fd, -1),), works)
+    receive()
+    stages(((fd, (0, -1)),), works)
+    ship(5)
+
+    for copies in started:
+        for sends, _, copy in copies:
+            pl.when(sends)(copy.wait_send)
+    for side, dz in ((0, 1), (1, -1)):
+        pl.when(has_z[dz])(tall_copy(side, dz).wait_send)
+    for k in order:
+        inward(me ^ k, me, me).wait_send()
+    for piece in range(6):
+        home(piece).wait()
+        for k in order:
+            outward(piece, me ^ k, me).wait_send()
+            outward(piece, me, me ^ k).wait_recv()
+
+
+def fused_body(peers, slabs, source, conductivity):
+    _, planes, rows, lanes = source.shape
+    block = rows // peers
+
+    def field(depth, width):
+        return pltpu.VMEM((depth, width, peers, lanes), jnp.float32)
+
+    large = field(planes + 2 * PAD, block + 2 * PAD)
+    small = field(planes // 2 + 2 * PAD2, block // 2 + 2 * PAD2)
+    dma = pltpu.SemaphoreType.DMA
+    anywhere = pl.BlockSpec(memory_space=pl.ANY)
+    shape = jax.ShapeDtypeStruct((planes, rows, lanes), jnp.float32)
+    solution, final_defect = pl.pallas_call(
+        functools.partial(cycle_kernel, peers, slabs),
+        out_shape=(shape, shape),
+        in_specs=[anywhere, anywhere],
+        out_specs=(anywhere, anywhere),
+        scratch_shapes=[
+            large, large, small, large,
+            large, small, large, large, small,
+            large, large, large, large, large, large,
+            large, large, large, large,
+            small, small, small, small,
+            pltpu.VMEM((planes, rows, lanes), jnp.float32),
+            pltpu.VMEM((planes + 4 * PAD2, rows, lanes), jnp.float32),
+            dma((peers,)), dma((peers,)), dma, dma((2,)),
+            dma((2,)), dma((2,)),
+            dma((6, 8)), dma((6, 8)),
+            dma((6, peers)), dma((6, peers)), dma((6,)),
+        ],
+        compiler_params=pltpu.CompilerParams(
+            collective_id=0, has_side_effects=True, vmem_limit_bytes=60 * 1024 * 1024
+        ),
+    )(source[0], conductivity)
+    return (solution[None], final_defect[None])
+
+
 def solution(mesh):
+    peers, slabs = mesh.shape["tm"], mesh.shape["space"]
+
+    def chosen(source, conductivity):
+        steps, planes, rows, lanes = source.shape
+        if fits(steps * peers, peers, slabs, planes, rows, lanes):
+            return fused_body(peers, slabs, source, conductivity)
+        return body(source, conductivity)
+
     return jax.shard_map(
-        body,
+        chosen,
         mesh=mesh,
         in_specs=(P("tm", "space", None, None), P("space", None, None)),
         out_specs=(P("tm", "space", None, None), P("tm", "space", None, None)),

time: 239 us -> 77.5 us (0.32); the launches traced: 235 us -> 77.4 us
  starting transfers between devices: 133 us -> 0 us
  Pallas kernels: 0 us -> 74 us
  waiting for transfers between devices: 67.7 us -> 0 us
  other arithmetic: 17.1 us -> 0 us
  local copies, waits for them, and re-layouts: 15.8 us -> 2.73 us
    ppermute x45 -> x0, starting transfers between devices: 133 us -> none  [the longest x15 65.6 us: shifted(): return lax.ppermute(shard, axis, pairs)]
    pallas_call x0 -> x1, Pallas kernels: none -> 74 us  [fused_body(): pl.pallas_call(functools.partial(cycle_kernel, peers, slabs), out_shape=(...]
    ppermute x45 -> x0, waiting for transfers between devices: 67.7 us -> none  [the longest x15 54.9 us: shifted(): return lax.ppermute(shard, axis, pairs)]
    slice x35 -> x0, local copies, waits for them, and re-layouts: 14.3 us -> none  [the longest x2 3.16 us: coarsen(): values[..., 1::2, 1::2, :]]
    add x11 -> x0, other arithmetic: 6.41 us -> none  [the longest x8 3.81 us: relaxed(): current + OMEGA * defect(current, right_side, earlier, padded, conduct, s...]
    concatenate x14 -> x0, other arithmetic: 5.63 us -> none  [padded_2(): shard = jnp.concatenate([before, shard, after], axis=dim)]
  transfers between devices with their start and end apart: 45 -> 0, of which waited for: 24 -> 0; matrix products, arithmetic and copies ran while one was open for 10% -> 0% of each run, Pallas kernels for 0% -> 0%
where the time goes in v3:
time: 77.5 us; the launch traced here: 77.4 us
  Pallas kernels  74 us (95%)
  local copies, waits for them, and re-layouts  2.73 us (4%)
    pallas_call x1, Pallas kernels, fused_body(): pl.pallas_call(functools.partial(cycle_kernel, peers, slabs), out_shape=(...  74 us
    unnamed x4, local copies, waits for them, and re-layouts  2.73 us

profile of v3, /device:TPU:0, one launch (start us, length us, event | category | flops | bytes accessed | tf_op | source)
XLA Modules:
  0.0 77.4 jit_solution(1575919785090921123)
XLA Ops:
  0.6 74.0 %shard_map.41 = (f32[8,128,128]{2,1,0:T(8,128)}, f32[8,128,128]{2,1,0:T(8,128)}) custom-call(f32[8,128,128]{2,1,0:T(8,128)} %bitcast.3, f32[8,128,128]{2,1,0:T(8,128)} %conduct_far.1), custom_call_target="tpu_custom_call" | custom-call | tf_op jit(solution)/shard_map/pallas_call | solution.py:608
  74.6 0.0 copy-start
  74.7 1.9 %copy.6 = f32[1,8,128,128]{3,2,1,0:T(8,128)} copy(f32[1,8,128,128]{3,2,1,0:T(8,128)} %bitcast.5) | data formatting | bytes 1048576
  76.6 0.0 copy-done
  76.6 0.8 %copy.7 = f32[1,8,128,128]{3,2,1,0:T(8,128)} copy(f32[1,8,128,128]{3,2,1,0:T(8,128)S(1)} %bitcast.4) | data formatting | bytes 1048576
Async XLA Ops:
  74.6 1.9 %copy-start = (f32[8,128,128]{2,1,0:T(8,128)S(1)}, f32[8,128,128]{2,1,0:T(8,128)}, u32[]{:S(2)}) copy-start(f32[8,128,128]{2,1,0:T(8,128)} %get-tuple-element.5) | copy-start | bytes 1572868

commit v4 on v3

--- a/solution.py
+++ b/solution.py
@@ -249,6 +249,10 @@
 
     def over(boxes, work):
         for z0, z1, x0, x1 in boxes:
+            if z1 - z0 <= 2 or x1 - x0 <= 4:
+                for z in range(z0, z1):
+                    work(z, x0, x1)
+                continue
 
             def step(z, _, x0=x0, x1=x1):
                 work(z, x0, x1)

time: 77.5 us -> 69.9 us (0.902)
  Pallas kernels: 74 us -> 66.4 us
    pallas_call x1, Pallas kernels: 74 us -> 66.4 us  [fused_body(): pl.pallas_call(functools.partial(cycle_kernel, peers, slabs), out_shape=(...]
where the time goes in v4:
time: 69.9 us; the launch traced here: 69.8 us
  Pallas kernels  66.4 us (95%)
  local copies, waits for them, and re-layouts  2.73 us (4%)
    pallas_call x1, Pallas kernels, fused_body(): pl.pallas_call(functools.partial(cycle_kernel, peers, slabs), out_shape=(...  66.4 us
    unnamed x4, local copies, waits for them, and re-layouts  2.73 us

profile of v4, /device:TPU:0, one launch (start us, length us, event | category | flops | bytes accessed | tf_op | source)
XLA Modules:
  0.0 69.8 jit_solution(9971952141769391489)
XLA Ops:
  0.6 66.4 %shard_map.41 = (f32[8,128,128]{2,1,0:T(8,128)}, f32[8,128,128]{2,1,0:T(8,128)}) custom-call(f32[8,128,128]{2,1,0:T(8,128)} %bitcast.3, f32[8,128,128]{2,1,0:T(8,128)} %conduct_far.1), custom_call_target="tpu_custom_call" | custom-call | tf_op jit(solution)/shard_map/pallas_call | solution.py:612
  67.0 0.0 copy-start
  67.0 1.9 %copy.6 = f32[1,8,128,128]{3,2,1,0:T(8,128)} copy(f32[1,8,128,128]{3,2,1,0:T(8,128)} %bitcast.5) | data formatting | bytes 1048576
  69.0 0.0 copy-done
  69.0 0.8 %copy.7 = f32[1,8,128,128]{3,2,1,0:T(8,128)} copy(f32[1,8,128,128]{3,2,1,0:T(8,128)S(1)} %bitcast.4) | data formatting | bytes 1048576
Async XLA Ops:
  67.0 1.9 %copy-start = (f32[8,128,128]{2,1,0:T(8,128)S(1)}, f32[8,128,128]{2,1,0:T(8,128)}, u32[]{:S(2)}) copy-start(f32[8,128,128]{2,1,0:T(8,128)} %get-tuple-element.5) | copy-start | bytes 1572868
